TPU v7x, 32 devices: a whole 2x2x4 slice. The times are simulated.
32 devices in a mesh: dp: 16 (over z, x, core), fsdp: 2 (over y).
Axes of the slice: x: 2, y: 2, z: 4, core: 2. Of those that a mesh axis runs over, the one named last changes fastest.
Arguments:
- patches: bfloat16 [64, 1024, 768], P(('dp', 'fsdp')), may hold values from -6 to 6
- ln_gain: bfloat16 [2, 768], P(None, 'fsdp'), may hold values from 0.25 to 1.75
- ln_bias: bfloat16 [2, 768], P(None, 'fsdp'), may hold values from -1.5 to 1.5
- w_qkv: bfloat16 [768, 2304], P('fsdp'), may hold values from -0.21875 to 0.21875
- b_qkv: bfloat16 [2304], P('fsdp'), may hold values from -1.5 to 1.5
- qk_gain: bfloat16 [2, 64], P(None, 'fsdp'), may hold values from 0.25 to 1.75
- w_proj: bfloat16 [768, 768], P('fsdp'), may hold values from -1.75 to 1.75
- out_bias: bfloat16 [2, 768], P(None, 'fsdp'), may hold values from -1.5 to 1.5
- w_in: bfloat16 [768, 3072], P('fsdp'), may hold values from -0.21875 to 0.21875
- b_in: bfloat16 [3072], P('fsdp'), may hold values from -1.5 to 1.5
- w_out: bfloat16 [3072, 768], P('fsdp'), may hold values from -0.109375 to 0.109375
- lengths: int32 [64, 10], P(('dp', 'fsdp')), may hold values from 0 to 1024, as said below
- cotangent: bfloat16 [64, 1024, 768], P(('dp', 'fsdp')), may hold values from -6 to 6
Outputs:
- block_out: bfloat16 [64, 1024, 768], P(('dp', 'fsdp'))
- grad_patches: float32 [64, 1024, 768], P(('dp', 'fsdp'))
- grad_ln_gain: float32 [2, 768], P(None, 'fsdp')
- grad_ln_bias: float32 [2, 768], P(None, 'fsdp')
- grad_w_qkv: float32 [768, 2304], P('fsdp')
- grad_b_qkv: float32 [2304], P('fsdp')
- grad_qk_gain: float32 [2, 64], P(None, 'fsdp')
- grad_w_proj: float32 [768, 768], P('fsdp')
- grad_out_bias: float32 [2, 768], P(None, 'fsdp')
- grad_w_in: float32 [768, 3072], P('fsdp')
- grad_b_in: float32 [3072], P('fsdp')
- grad_w_out: float32 [3072, 768], P('fsdp')
Inputs may be any that keep to these rules, and one draw needn't show every extreme that they name: In each row the nonzero lengths come first, each from 100 to 1024, and together they are at most 1024; the remaining entries are 0. The first row holds a single picture of 1024 patches.
All inputs are finite; a program needn't handle non-finite values.
Results may differ from a plain program's by a relative error of at most 0.019.
Values may be sent and summed in bfloat16 or wider, within the bound.
A program may use at most 384 MiB of HBM per device.

v0:
```python
import math

import jax
import jax.numpy as jnp
from jax import lax
from jax.sharding import PartitionSpec as P

H = 12


def normalize(values, gain, shift):
    average = jnp.mean(values, axis=-1, keepdims=True)
    centered = values - average
    variance = jnp.mean(centered * centered, axis=-1, keepdims=True)
    return centered * lax.rsqrt(variance + 1e-06) * gain + shift


def head_norm(values, gain):
    return normalize(values, gain, 0.0)


def picture_ids(row_lengths, row_len):
    pic_ends = jnp.cumsum(row_lengths)
    positions = jnp.arange(row_len, dtype=jnp.int32)
    pic_id = jnp.sum((positions[:, None] >= pic_ends[None, :]).astype(jnp.int32), axis=1)
    inside = (positions < pic_ends[row_lengths.shape[0] - 1]).astype(jnp.float32)
    return (pic_id, inside)


def masked_scores(query_block, keys_low, pic_block, pic_id, scale):
    scores = (
        jnp.einsum("qhd,khd->hqk", query_block, keys_low, preferred_element_type=jnp.float32)
        * scale
    )
    same_pic = pic_block[:, None] == pic_id[None, :]
    return jnp.where(same_pic[None], scores, -1e30)


def attend(queries, keys_low, values_low, pic_id, block, scale):
    pieces = []
    log_totals = []
    for start in range(0, queries.shape[0], block):
        scores = masked_scores(
            queries[start : start + block], keys_low, pic_id[start : start + block], pic_id, scale
        )
        row_max = jnp.max(scores, axis=-1, keepdims=True)
        exp_scores = jnp.exp(scores - row_max)
        total = jnp.sum(exp_scores, axis=-1, keepdims=True)
        probs = exp_scores / total
        pieces.append(
            jnp.einsum(
                "hqk,khd->qhd",
                probs.astype(jnp.bfloat16),
                values_low,
                preferred_element_type=jnp.float32,
            )
        )
        log_totals.append(row_max + jnp.log(total))
    return (jnp.concatenate(pieces, axis=0), jnp.concatenate(log_totals, axis=1))


def attend_back(queries, keys_low, values_low, pic_id, log_total, grad_attn, block, scale):
    grad_keys = jnp.zeros(keys_low.shape, jnp.float32)
    grad_values = jnp.zeros(values_low.shape, jnp.float32)
    grad_query_parts = []
    for start in range(0, queries.shape[0], block):
        query_block = queries[start : start + block]
        grad_block = grad_attn[start : start + block]
        scores = masked_scores(query_block, keys_low, pic_id[start : start + block], pic_id, scale)
        probs = jnp.exp(scores - log_total[:, start : start + block])
        grad_probs = jnp.einsum(
            "qhd,khd->hqk", grad_block, values_low, preferred_element_type=jnp.float32
        )
        centre = jnp.sum(probs * grad_probs, axis=-1, keepdims=True)
        grad_scores = (probs * (grad_probs - centre) * scale).astype(jnp.bfloat16)
        grad_query_parts.append(
            jnp.einsum("hqk,khd->qhd", grad_scores, keys_low, preferred_element_type=jnp.float32)
        )
        grad_keys = grad_keys + jnp.einsum(
            "hqk,qhd->khd", grad_scores, query_block, preferred_element_type=jnp.float32
        )
        grad_values = grad_values + jnp.einsum(
            "hqk,qhd->khd",
            probs.astype(jnp.bfloat16),
            grad_block,
            preferred_element_type=jnp.float32,
        )
    return (jnp.concatenate(grad_query_parts, axis=0), grad_keys, grad_values)


def forward_row(row_patches, pic_id, full_params):
    ln_gain, ln_bias, w_qkv, b_qkv, qk_gain, w_proj, out_bias, w_in, b_in, w_out = full_params
    row_len, width = row_patches.shape
    head_dim = width // H
    scale = 1.0 / math.sqrt(head_dim)
    block = min(512, row_len)
    source = row_patches.astype(jnp.float32)
    normed1 = normalize(
        source, ln_gain[0].astype(jnp.float32), ln_bias[0].astype(jnp.float32)
    ).astype(jnp.bfloat16)
    proj = jnp.dot(normed1, w_qkv, preferred_element_type=jnp.float32) + b_qkv.astype(jnp.float32)
    proj = proj.reshape(row_len, 3, H, head_dim)
    queries = head_norm(proj[:, 0], qk_gain[0].astype(jnp.float32)).astype(jnp.bfloat16)
    keys_low = head_norm(proj[:, 1], qk_gain[1].astype(jnp.float32)).astype(jnp.bfloat16)
    values_low = proj[:, 2].astype(jnp.bfloat16)
    attn_heads, log_total = attend(queries, keys_low, values_low, pic_id, block, scale)
    attn = attn_heads.reshape(row_len, width).astype(jnp.bfloat16)
    resid = (
        source
        + jnp.dot(attn, w_proj, preferred_element_type=jnp.float32)
        + out_bias[0].astype(jnp.float32)
    )
    normed2 = normalize(
        resid, ln_gain[1].astype(jnp.float32), ln_bias[1].astype(jnp.float32)
    ).astype(jnp.bfloat16)
    hidden = jnp.dot(normed2, w_in, preferred_element_type=jnp.float32) + b_in.astype(jnp.float32)
    activated = jax.nn.gelu(hidden).astype(jnp.bfloat16)
    result = (
        resid
        + jnp.dot(activated, w_out, preferred_element_type=jnp.float32)
        + out_bias[1].astype(jnp.float32)
    )
    kept = (
        source,
        proj,
        queries,
        keys_low,
        values_low,
        log_total,
        attn,
        resid,
        normed1,
        normed2,
        hidden,
        activated,
    )
    return (result.astype(jnp.bfloat16), kept)


def backward_row(row_cot, pic_id, inside, kept, full_params):
    ln_gain, ln_bias, w_qkv, b_qkv, qk_gain, w_proj, out_bias, w_in, b_in, w_out = full_params
    (
        source,
        proj,
        queries,
        keys_low,
        values_low,
        log_total,
        attn,
        resid,
        normed1,
        normed2,
        hidden,
        activated,
    ) = kept
    row_len, width = source.shape
    head_dim = width // H
    scale = 1.0 / math.sqrt(head_dim)
    block = min(512, row_len)
    grad_y = row_cot.astype(jnp.float32) * inside[:, None]
    grad_mlp = grad_y.astype(jnp.bfloat16)
    grad_w_out = jnp.einsum("tf,td->fd", activated, grad_mlp, preferred_element_type=jnp.float32)
    grad_bias_mlp = jnp.sum(grad_mlp.astype(jnp.float32), axis=0)
    grad_act = jnp.einsum("td,fd->tf", grad_mlp, w_out, preferred_element_type=jnp.float32)
    gelu_out, gelu_pull = jax.vjp(jax.nn.gelu, hidden)
    grad_hidden = gelu_pull(grad_act)[0].astype(jnp.bfloat16)
    grad_w_in = jnp.einsum("td,tf->df", normed2, grad_hidden, preferred_element_type=jnp.float32)
    grad_b_in = jnp.sum(grad_hidden.astype(jnp.float32), axis=0)
    grad_norm2 = jnp.einsum("tf,df->td", grad_hidden, w_in, preferred_element_type=jnp.float32)
    norm_out, norm_pull = jax.vjp(
        normalize, resid, ln_gain[1].astype(jnp.float32), ln_bias[1].astype(jnp.float32)
    )
    grad_resid_ln, grad_gain_two, grad_shift_two = norm_pull(grad_norm2)
    grad_resid = grad_y + grad_resid_ln
    grad_branch = grad_resid.astype(jnp.bfloat16)
    grad_w_proj = jnp.einsum("td,te->de", attn, grad_branch, preferred_element_type=jnp.float32)
    grad_bias_attn = jnp.sum(grad_branch.astype(jnp.float32), axis=0)
    grad_attn = jnp.einsum("te,de->td", grad_branch, w_proj, preferred_element_type=jnp.float32)
    grad_attn = grad_attn.astype(jnp.bfloat16).reshape(row_len, H, head_dim)
    grad_queries, grad_keys, grad_values = attend_back(
        queries, keys_low, values_low, pic_id, log_total, grad_attn, block, scale
    )
    query_out, query_pull = jax.vjp(head_norm, proj[:, 0], qk_gain[0].astype(jnp.float32))
    grad_query_raw, grad_query_gain = query_pull(grad_queries)
    key_out, key_pull = jax.vjp(head_norm, proj[:, 1], qk_gain[1].astype(jnp.float32))
    grad_key_raw, grad_key_gain = key_pull(grad_keys)
    grad_proj = (
        jnp.stack([grad_query_raw, grad_key_raw, grad_values], axis=1)
        .reshape(row_len, 3 * width)
        .astype(jnp.bfloat16)
    )
    grad_w_qkv = jnp.einsum("td,te->de", normed1, grad_proj, preferred_element_type=jnp.float32)
    grad_b_qkv = jnp.sum(grad_proj.astype(jnp.float32), axis=0)
    grad_norm1 = jnp.einsum("te,de->td", grad_proj, w_qkv, preferred_element_type=jnp.float32)
    first_out, first_pull = jax.vjp(
        normalize, source, ln_gain[0].astype(jnp.float32), ln_bias[0].astype(jnp.float32)
    )
    grad_source_ln, grad_gain_one, grad_shift_one = first_pull(grad_norm1)
    grad_input = grad_resid + grad_source_ln
    grads = (
        jnp.stack([grad_gain_one, grad_gain_two]),
        jnp.stack([grad_shift_one, grad_shift_two]),
        grad_w_qkv,
        grad_b_qkv,
        jnp.stack([grad_query_gain, grad_key_gain]),
        grad_w_proj,
        jnp.stack([grad_bias_attn, grad_bias_mlp]),
        grad_w_in,
        grad_b_in,
        grad_w_out,
    )
    return (grad_input, grads)


def on_device(
    patches,
    ln_gain,
    ln_bias,
    w_qkv,
    b_qkv,
    qk_gain,
    w_proj,
    out_bias,
    w_in,
    b_in,
    w_out,
    lengths,
    cotangent,
):
    micro, row_len, width = patches.shape

    def micro_step(index, carry):
        totals, outs_all, grads_all = carry
        row_patches = lax.dynamic_index_in_dim(patches, index, 0, keepdims=False)
        row_lengths = lax.dynamic_index_in_dim(lengths, index, 0, keepdims=False)
        row_cot = lax.dynamic_index_in_dim(cotangent, index, 0, keepdims=False)
        pic_id, inside = picture_ids(row_lengths, row_len)
        full_fwd = (
            lax.all_gather(ln_gain, "fsdp", axis=1, tiled=True),
            lax.all_gather(ln_bias, "fsdp", axis=1, tiled=True),
            lax.all_gather(w_qkv, "fsdp", axis=0, tiled=True),
            lax.all_gather(b_qkv, "fsdp", axis=0, tiled=True),
            lax.all_gather(qk_gain, "fsdp", axis=1, tiled=True),
            lax.all_gather(w_proj, "fsdp", axis=0, tiled=True),
            lax.all_gather(out_bias, "fsdp", axis=1, tiled=True),
            lax.all_gather(w_in, "fsdp", axis=0, tiled=True),
            lax.all_gather(b_in, "fsdp", axis=0, tiled=True),
            lax.all_gather(w_out, "fsdp", axis=0, tiled=True),
        )
        result, kept = forward_row(row_patches, pic_id, full_fwd)
        full_bwd = (
            lax.all_gather(ln_gain, "fsdp", axis=1, tiled=True),
            lax.all_gather(ln_bias, "fsdp", axis=1, tiled=True),
            lax.all_gather(w_qkv, "fsdp", axis=0, tiled=True),
            lax.all_gather(b_qkv, "fsdp", axis=0, tiled=True),
            lax.all_gather(qk_gain, "fsdp", axis=1, tiled=True),
            lax.all_gather(w_proj, "fsdp", axis=0, tiled=True),
            lax.all_gather(out_bias, "fsdp", axis=1, tiled=True),
            lax.all_gather(w_in, "fsdp", axis=0, tiled=True),
            lax.all_gather(b_in, "fsdp", axis=0, tiled=True),
            lax.all_gather(w_out, "fsdp", axis=0, tiled=True),
        )
        grad_input, grads = backward_row(row_cot, pic_id, inside, kept, full_bwd)
        totals = jax.tree.map(lambda first, second: first + second, totals, grads)
        outs_all = lax.dynamic_update_index_in_dim(outs_all, result, index, 0)
        grads_all = lax.dynamic_update_index_in_dim(grads_all, grad_input, index, 0)
        return (totals, outs_all, grads_all)

    full_shapes = (
        (2, width),
        (2, width),
        (width, 3 * width),
        (3 * width,),
        (2, width // H),
        (width, width),
        (2, width),
        (width, w_in.shape[1]),
        (w_in.shape[1],),
        (w_in.shape[1], width),
    )
    zeros_init = tuple((jnp.zeros(shape_item, jnp.float32) for shape_item in full_shapes))
    outs_init = jnp.zeros((micro, row_len, width), jnp.bfloat16)
    grads_init = jnp.zeros((micro, row_len, width), jnp.float32)
    totals, outs_all, grads_all = lax.fori_loop(
        0, micro, micro_step, (zeros_init, outs_init, grads_init)
    )
    g_gain, g_shift, g_qkv, g_bqkv, g_qk, g_proj, g_obias, g_win, g_bin, g_wout = totals
    shard_sums = (
        lax.psum_scatter(
            g_gain.astype(jnp.bfloat16), "fsdp", scatter_dimension=1, tiled=True
        ).astype(jnp.float32),
        lax.psum_scatter(
            g_shift.astype(jnp.bfloat16), "fsdp", scatter_dimension=1, tiled=True
        ).astype(jnp.float32),
        lax.psum_scatter(
            g_qkv.astype(jnp.bfloat16), "fsdp", scatter_dimension=0, tiled=True
        ).astype(jnp.float32),
        lax.psum_scatter(
            g_bqkv.astype(jnp.bfloat16), "fsdp", scatter_dimension=0, tiled=True
        ).astype(jnp.float32),
        lax.psum_scatter(g_qk.astype(jnp.bfloat16), "fsdp", scatter_dimension=1, tiled=True).astype(
            jnp.float32
        ),
        lax.psum_scatter(
            g_proj.astype(jnp.bfloat16), "fsdp", scatter_dimension=0, tiled=True
        ).astype(jnp.float32),
        lax.psum_scatter(
            g_obias.astype(jnp.bfloat16), "fsdp", scatter_dimension=1, tiled=True
        ).astype(jnp.float32),
        lax.psum_scatter(
            g_win.astype(jnp.bfloat16), "fsdp", scatter_dimension=0, tiled=True
        ).astype(jnp.float32),
        lax.psum_scatter(
            g_bin.astype(jnp.bfloat16), "fsdp", scatter_dimension=0, tiled=True
        ).astype(jnp.float32),
        lax.psum_scatter(
            g_wout.astype(jnp.bfloat16), "fsdp", scatter_dimension=0, tiled=True
        ).astype(jnp.float32),
    )
    s_gain, s_shift, s_qkv, s_bqkv, s_qk, s_proj, s_obias, s_win, s_bin, s_wout = shard_sums
    summed = (
        lax.psum(s_gain.astype(jnp.bfloat16), "dp").astype(jnp.float32),
        lax.psum(s_shift.astype(jnp.bfloat16), "dp").astype(jnp.float32),
        lax.psum(s_qkv.astype(jnp.bfloat16), "dp").astype(jnp.float32),
        lax.psum(s_bqkv.astype(jnp.bfloat16), "dp").astype(jnp.float32),
        lax.psum(s_qk.astype(jnp.bfloat16), "dp").astype(jnp.float32),
        lax.psum(s_proj.astype(jnp.bfloat16), "dp").astype(jnp.float32),
        lax.psum(s_obias.astype(jnp.bfloat16), "dp").astype(jnp.float32),
        lax.psum(s_win.astype(jnp.bfloat16), "dp").astype(jnp.float32),
        lax.psum(s_bin.astype(jnp.bfloat16), "dp").astype(jnp.float32),
        lax.psum(s_wout.astype(jnp.bfloat16), "dp").astype(jnp.float32),
    )
    return (
        outs_all,
        grads_all,
        summed[0],
        summed[1],
        summed[2],
        summed[3],
        summed[4],
        summed[5],
        summed[6],
        summed[7],
        summed[8],
        summed[9],
    )


def solution(mesh):
    placed = (
        P(("dp", "fsdp"), None, None),
        P(None, "fsdp"),
        P(None, "fsdp"),
        P("fsdp", None),
        P("fsdp"),
        P(None, "fsdp"),
        P("fsdp", None),
        P(None, "fsdp"),
        P("fsdp", None),
        P("fsdp"),
        P("fsdp", None),
        P(("dp", "fsdp"), None),
        P(("dp", "fsdp"), None, None),
    )
    return jax.shard_map(
        on_device,
        mesh=mesh,
        in_specs=placed,
        out_specs=(
            P(("dp", "fsdp"), None, None),
            P(("dp", "fsdp"), None, None),
            P(None, "fsdp"),
            P(None, "fsdp"),
            P("fsdp", None),
            P("fsdp"),
            P(None, "fsdp"),
            P("fsdp", None),
            P(None, "fsdp"),
            P("fsdp", None),
            P("fsdp"),
            P("fsdp", None),
        ),
        check_vma=False,
    )
```

profile of v0, /device:TPU:1, one launch (start us, length us, event | category | flops | bytes accessed | tf_op | source)
XLA Modules:
  0.0 1641.6 jit_solution(3895694325186861276)
XLA Ops:
  8.1 1206.8 %while.38 = (s32[]{:T(128)}, f32[2,768]{1,0:T(2,128)}, f32[2,768]{1,0:T(2,128)}, f32[768,2304]{1,0:T(8,128)}, f32[2304]{0:T(1024)}, /*index=5*/f32[2,64]{1,0:T(2...) while((s32[]{:T(128)}, f32[2,768]{1,0:T(2,128)}, ...), condition=%wide.region_35.36_spmd.clone, body=%wide.region_0.35_spmd.clone.sunk | while | flops 53925380096 | bytes 1466752000 | solution.py:284
  44.1 18.2 %all-gather.19.cloned.1.call-done = bf16[768,2304]{1,0:T(8,128)(2,1)} async-done(((bf16[384,2304]{1,0:T(8,128)(2,1)}), bf16[768,2304]{1,0:T(8,128)(2,1)}) %all-gather.19.cloned.1.call-update) | async-done | bytes 3538960 | tf_op jit(solution)/shard_map/while/body/eval_jaxpr/all_gather | solution.py:241
  182.7 32.3 %all-gather.23.cloned.1.call-done = bf16[3072,768]{1,0:T(8,128)(2,1)} async-done(((bf16[1536,768]{1,0:T(8,128)(2,1)}), bf16[3072,768]{1,0:T(8,128)(2,1)}) %all-gather.23.cloned.1.call-update) | async-done | bytes 4718608 | tf_op jit(solution)/shard_map/while/body/eval_jaxpr/all_gather | solution.py:261
  215.0 16.4 convert_reduce_fusion.16
  263.1 52.0 %fusion.310 = f32[12,64,512]{2,1,0:T(8,128)} fusion(bf16[1024,12,64]{0,2,1:T(8,128)(2,1)} %copy-done.13, f32[12,512,1024]{2,1,0:T(8,128)} %fusion.309, f32[12,512]{1,0:T(8,128)S(1)} %log_add_fusion.5, f32[12,512,1024]{2,1,0:T(8,128)} %get-tuple-element.1204, pred[512,1024]{1,0:T(8,128)(4,1)} %copy-done.25), kind=kOutput, calls=%fused_computation.38.clone.1 | convolution fusion | flops 874519552 | bytes 54026240 | tf_op jit(solution)/shard_map/while/body/eval_jaxpr/hqk,khd->qhd/dot_general | solution.py:77
  315.1 54.2 %fusion.311 = f32[12,64,1024]{2,1,0:T(8,128)} fusion(f32[12,512,1024]{2,1,0:T(8,128)} %fusion.309, f32[12,512]{1,0:T(8,128)S(1)} %log_add_fusion.5, f32[12,512,1024]{2,1,0:T(8,128)} %get-tuple-element.1204, pred[512,1024]{1,0:T(8,128)(4,1)} %copy-done.25, bf16[1024,12,64]{0,2,1:T(8,128)(2,1)} %copy-done.18), kind=kOutput, calls=%fused_computation.37.clone.1 | convolution fusion | flops 874519552 | bytes 105709568 | tf_op jit(solution)/shard_map/while/body/eval_jaxpr/hqk,qhd->khd/dot_general | solution.py:79
  383.7 14.8 select_add_fusion.17
  434.3 13.2 add_bitcast_fusion.6
  447.5 51.9 %fusion.308 = f32[12,64,512]{2,1,0:T(8,128)} fusion(bf16[1024,12,64]{0,2,1:T(8,128)(2,1)S(1)} %copy-done.14, f32[12,512,1024]{2,1,0:T(8,128)} %fusion.307, f32[12,512]{1,0:T(8,128)S(1)} %copy-done.62, f32[12,512,1024]{2,1,0:T(8,128)} %get-tuple-element.1201, pred[512,1024]{1,0:T(8,128)(4,1)} %copy-done.23), kind=kOutput, calls=%fused_computation.40.clone.1 | convolution fusion | flops 874519552 | bytes 54026240 | tf_op jit(solution)/shard_map/while/body/eval_jaxpr/hqk,khd->qhd/dot_general | solution.py:77
  502.8 57.5 %multiply_reduce_fusion.19 = (f32[64]{0:T(128)}, f32[1024,12]{0,1:T(8,128)}, f32[1024,12]{0,1:T(8,128)}, f32[12,64,1024]{2,1,0:T(8,128)S(1)}) fusion(f32[512,12,64]{0,2,1:T(8,128)} %bitcast.338, f32[512,12,64]{0,2,1:T(8,128)} %bitcast.334, f32[1024,3,12,64]{0,3,2,1:T(8,128)} %bitcast.317, f32[1024,12]{0,1:T(8,128)S(1)} %copy-done.40, ...), kind=kOutput, calls=%fused_computation.91.clone.1 | convolution fusion | flops 887077824 | bytes 118588672 | tf_op jit(solution)/shard_map/while/body/eval_jaxpr/hqk,qhd->khd/dot_general | solution.py:79
  644.0 16.8 %all-gather.19.cloned.1.call-done = bf16[768,2304]{1,0:T(8,128)(2,1)} async-done(((bf16[384,2304]{1,0:T(8,128)(2,1)}), bf16[768,2304]{1,0:T(8,128)(2,1)}) %all-gather.19.cloned.1.call-update) | async-done | bytes 3538960 | tf_op jit(solution)/shard_map/while/body/eval_jaxpr/all_gather | solution.py:241
  780.8 32.6 %all-gather.23.cloned.1.call-done = bf16[3072,768]{1,0:T(8,128)(2,1)} async-done(((bf16[1536,768]{1,0:T(8,128)(2,1)}), bf16[3072,768]{1,0:T(8,128)(2,1)}) %all-gather.23.cloned.1.call-update) | async-done | bytes 4718608 | tf_op jit(solution)/shard_map/while/body/eval_jaxpr/all_gather | solution.py:261
  813.4 16.4 convert_reduce_fusion.16
  861.5 52.0 %fusion.310 = f32[12,64,512]{2,1,0:T(8,128)} fusion(bf16[1024,12,64]{0,2,1:T(8,128)(2,1)} %copy-done.13, f32[12,512,1024]{2,1,0:T(8,128)} %fusion.309, f32[12,512]{1,0:T(8,128)S(1)} %log_add_fusion.5, f32[12,512,1024]{2,1,0:T(8,128)} %get-tuple-element.1204, pred[512,1024]{1,0:T(8,128)(4,1)} %copy-done.25), kind=kOutput, calls=%fused_computation.38.clone.1 | convolution fusion | flops 874519552 | bytes 54026240 | tf_op jit(solution)/shard_map/while/body/eval_jaxpr/hqk,khd->qhd/dot_general | solution.py:77
  913.5 54.2 %fusion.311 = f32[12,64,1024]{2,1,0:T(8,128)} fusion(f32[12,512,1024]{2,1,0:T(8,128)} %fusion.309, f32[12,512]{1,0:T(8,128)S(1)} %log_add_fusion.5, f32[12,512,1024]{2,1,0:T(8,128)} %get-tuple-element.1204, pred[512,1024]{1,0:T(8,128)(4,1)} %copy-done.25, bf16[1024,12,64]{0,2,1:T(8,128)(2,1)} %copy-done.18), kind=kOutput, calls=%fused_computation.37.clone.1 | convolution fusion | flops 874519552 | bytes 105709568 | tf_op jit(solution)/shard_map/while/body/eval_jaxpr/hqk,qhd->khd/dot_general | solution.py:79
  982.1 16.1 select_add_fusion.17
  1035.4 13.2 add_bitcast_fusion.6
  1048.6 51.9 %fusion.308 = f32[12,64,512]{2,1,0:T(8,128)} fusion(bf16[1024,12,64]{0,2,1:T(8,128)(2,1)S(1)} %copy-done.14, f32[12,512,1024]{2,1,0:T(8,128)} %fusion.307, f32[12,512]{1,0:T(8,128)S(1)} %copy-done.62, f32[12,512,1024]{2,1,0:T(8,128)} %get-tuple-element.1201, pred[512,1024]{1,0:T(8,128)(4,1)} %copy-done.23), kind=kOutput, calls=%fused_computation.40.clone.1 | convolution fusion | flops 874519552 | bytes 54026240 | tf_op jit(solution)/shard_map/while/body/eval_jaxpr/hqk,khd->qhd/dot_general | solution.py:77
  1104.0 57.5 %multiply_reduce_fusion.19 = (f32[64]{0:T(128)}, f32[1024,12]{0,1:T(8,128)}, f32[1024,12]{0,1:T(8,128)}, f32[12,64,1024]{2,1,0:T(8,128)S(1)}) fusion(f32[512,12,64]{0,2,1:T(8,128)} %bitcast.338, f32[512,12,64]{0,2,1:T(8,128)} %bitcast.334, f32[1024,3,12,64]{0,3,2,1:T(8,128)} %bitcast.317, f32[1024,12]{0,1:T(8,128)S(1)} %copy-done.40, ...), kind=kOutput, calls=%fused_computation.91.clone.1 | convolution fusion | flops 887077824 | bytes 118588672 | tf_op jit(solution)/shard_map/while/body/eval_jaxpr/hqk,qhd->khd/dot_general | solution.py:79
  1240.8 49.5 %reduce-scatter.17.cloned.1.call-done = bf16[384,2304]{1,0:T(8,128)(2,1)} async-done(((bf16[768,2304]{1,0:T(8,128)(2,1)}), bf16[384,2304]{1,0:T(8,128)(2,1)}) %reduce-scatter.17.cloned.1.call-update) | async-done | bytes 1769488 | tf_op jit(solution)/shard_map/reduce_scatter | solution.py:295
  1290.3 62.8 %reduce-scatter.21.cloned.1.call-done = bf16[384,3072]{1,0:T(8,128)(2,1)} async-done(((bf16[768,3072]{1,0:T(8,128)(2,1)}), bf16[384,3072]{1,0:T(8,128)(2,1)}) %reduce-scatter.21.cloned.1.call-update) | async-done | bytes 2359312 | tf_op jit(solution)/shard_map/reduce_scatter | solution.py:310
  1353.1 62.9 %reduce-scatter.23.cloned.1.call-done = bf16[1536,768]{1,0:T(8,128)(2,1)} async-done(((bf16[3072,768]{1,0:T(8,128)(2,1)}), bf16[1536,768]{1,0:T(8,128)(2,1)}) %reduce-scatter.23.cloned.1.call-update) | async-done | bytes 2359312 | tf_op jit(solution)/shard_map/reduce_scatter | solution.py:316
  1468.7 59.5 %all-reduce.2 = (bf16[2,384]{1,0:T(2,128)(2,1)S(1)}, bf16[2,384]{1,0:T(2,128)(2,1)S(1)}, bf16[1152]{0:T(1024)(128)(2,1)S(1)}, bf16[2,32]{1,0:T(2,128)(2,1)S(1)},...) all-reduce(bf16[2,384]{1,0:T(2,128)(2,1)S(1)} %copy.73, ...), channel_id=1, replica_groups=mesh['dp'=16,'fsdp'=2] {'dp'}, use_global_device_ids=true, to_apply=%region_37.38 | all-reduce | flops 5056 | bytes 20224 | tf_op jit(solution)/shard_map/psum | solution.py:322
  1531.7 90.9 %all-reduce.7.cloned.1.call-done = (bf16[384,2304]{1,0:T(8,128)(2,1)}, bf16[384,768]{1,0:T(8,128)(2,1)}, bf16[384,3072]{1,0:T(8,128)(2,1)}, bf16[1536,768]{1,0:T(8,128)(2,1)}) async-done(((bf16[384,2304]{1,0:T(8,128)(2,1)}, bf16[384,768]{1,0:T(8,128)(2,1)}, bf16[384,3072]{1,0:T(8,128)(2,1)}, bf16[1536,768]{1,0:T(8,128)(2,1)}), (bf16[384,2304]{1,0:T(8,128)(2,1)}, bf16[384,768]{1,0:T(8,128)(2,1)}, ...) | async-done | bytes 7077904 | tf_op jit(solution)/shard_map/psum | solution.py:324
  (723 shorter events, 670.2 us)
Async XLA Ops:
  8.4 53.9 %all-gather.19.cloned.1.call-start = ((), (), s32[]{:S(2)}) async-start(), calls=%async_computation.18 | async-start | bytes 5308416 | tf_op jit(solution)/shard_map/while/body/eval_jaxpr/all_gather | solution.py:241
  9.1 154.6 %all-gather.21.cloned.1.call-start = ((), (), s32[]{:S(2)}) async-start(), calls=%async_computation.19 | async-start | bytes 1769472 | tf_op jit(solution)/shard_map/while/body/eval_jaxpr/all_gather | solution.py:244
  9.9 161.5 %all-gather.17.cloned.1.call-start = ((), (), s32[]{:S(2)}) async-start(), calls=%async_computation.17 | async-start | bytes 7077888 | tf_op jit(solution)/shard_map/while/body/eval_jaxpr/all_gather | solution.py:246
  10.6 204.3 %all-gather.23.cloned.1.call-start = ((), (), s32[]{:S(2)}) async-start(), calls=%async_computation.20 | async-start | bytes 7077888 | tf_op jit(solution)/shard_map/while/body/eval_jaxpr/all_gather | solution.py:261
  15.8 74.1 %copy-start.80 = (f32[64]{0:T(128)}, f32[64]{0:T(128)S(1)}, u32[]{:S(2)}) copy-start(f32[64]{0:T(128)S(1)} %get-tuple-element.1193) | copy-start | bytes 772 | tf_op jit(solution)/shard_map/while
  15.8 74.1 %copy-start.83 = (f32[64]{0:T(128)}, f32[64]{0:T(128)S(1)}, u32[]{:S(2)}) copy-start(f32[64]{0:T(128)S(1)} %get-tuple-element.1197) | copy-start | bytes 772 | tf_op jit(solution)/shard_map/while
  44.1 71.7 %copy-start.25 = (pred[512,1024]{1,0:T(8,128)(4,1)}, pred[512,1024]{1,0:T(8,128)(4,1)S(1)}, u32[]{:S(2)}) copy-start(pred[512,1024]{1,0:T(8,128)(4,1)S(1)} %get-tuple-element.1203) | copy-start | bytes 1572868 | tf_op jit(solution)/shard_map/while
  44.1 106.8 %copy-start.23 = (pred[512,1024]{1,0:T(8,128)(4,1)}, pred[512,1024]{1,0:T(8,128)(4,1)S(1)}, u32[]{:S(2)}) copy-start(pred[512,1024]{1,0:T(8,128)(4,1)S(1)} %get-tuple-element.1190) | copy-start | bytes 1572868 | tf_op jit(solution)/shard_map/while
  609.0 51.7 %all-gather.19.cloned.1.call-start = ((), (), s32[]{:S(2)}) async-start(), calls=%async_computation.18 | async-start | bytes 5308416 | tf_op jit(solution)/shard_map/while/body/eval_jaxpr/all_gather | solution.py:241
  609.7 152.3 %all-gather.21.cloned.1.call-start = ((), (), s32[]{:S(2)}) async-start(), calls=%async_computation.19 | async-start | bytes 1769472 | tf_op jit(solution)/shard_map/while/body/eval_jaxpr/all_gather | solution.py:244
  610.2 159.2 %all-gather.17.cloned.1.call-start = ((), (), s32[]{:S(2)}) async-start(), calls=%async_computation.17 | async-start | bytes 7077888 | tf_op jit(solution)/shard_map/while/body/eval_jaxpr/all_gather | solution.py:246
  611.0 202.4 %all-gather.23.cloned.1.call-start = ((), (), s32[]{:S(2)}) async-start(), calls=%async_computation.20 | async-start | bytes 7077888 | tf_op jit(solution)/shard_map/while/body/eval_jaxpr/all_gather | solution.py:261
  615.7 72.6 %copy-start.80 = (f32[64]{0:T(128)}, f32[64]{0:T(128)S(1)}, u32[]{:S(2)}) copy-start(f32[64]{0:T(128)S(1)} %get-tuple-element.1193) | copy-start | bytes 772 | tf_op jit(solution)/shard_map/while
  615.7 72.6 %copy-start.83 = (f32[64]{0:T(128)}, f32[64]{0:T(128)S(1)}, u32[]{:S(2)}) copy-start(f32[64]{0:T(128)S(1)} %get-tuple-element.1197) | copy-start | bytes 772 | tf_op jit(solution)/shard_map/while
  644.0 105.1 %copy-start.23 = (pred[512,1024]{1,0:T(8,128)(4,1)}, pred[512,1024]{1,0:T(8,128)(4,1)S(1)}, u32[]{:S(2)}) copy-start(pred[512,1024]{1,0:T(8,128)(4,1)S(1)} %get-tuple-element.1190) | copy-start | bytes 1572868 | tf_op jit(solution)/shard_map/while
  1214.9 25.9 %reduce-scatter.19.cloned.1.call-start = ((), (), s32[]{:S(2)}) async-start(), calls=%async_computation.9 | async-start | bytes 1769472 | tf_op jit(solution)/shard_map/reduce_scatter | solution.py:304
  1217.8 72.6 %reduce-scatter.17.cloned.1.call-start = ((), (), s32[]{:S(2)}) async-start(), calls=%async_computation.8 | async-start | bytes 5308416 | tf_op jit(solution)/shard_map/reduce_scatter | solution.py:295
  1223.0 130.1 %reduce-scatter.21.cloned.1.call-start = ((), (), s32[]{:S(2)}) async-start(), calls=%async_computation.10 | async-start | bytes 7077888 | tf_op jit(solution)/shard_map/reduce_scatter | solution.py:310
  1230.1 186.0 %reduce-scatter.23.cloned.1.call-start = ((), (), s32[]{:S(2)}) async-start(), calls=%async_computation.11 | async-start | bytes 7077888 | tf_op jit(solution)/shard_map/reduce_scatter | solution.py:316
  1236.5 191.4 %reduce-scatter.29.cloned.1.call-start = ((), (), s32[]{:S(2)}) async-start(), calls=%async_computation.14 | async-start | bytes 24576
  1237.9 203.6 %reduce-scatter.31.cloned.1.call-start = ((), (), s32[]{:S(2)}) async-start(), calls=%async_computation.15 | async-start | bytes 294912
  1238.8 215.8 %reduce-scatter.27.cloned.1.call-start = ((), (), s32[]{:S(2)}) async-start(), calls=%async_computation.13 | async-start | bytes 294912
  1239.8 227.9 %reduce-scatter.25.cloned.1.call-start = ((), (), s32[]{:S(2)}) async-start(), calls=%async_computation.12 | async-start | bytes 294912
  1240.7 381.9 %all-reduce.7.cloned.1.call-start = ((), (), s32[]{:S(2)}) async-start(), calls=%async_computation.16 | async-start | bytes 14155776 | tf_op jit(solution)/shard_map/psum | solution.py:324
  (206 other events, 2374.4 us)
Sparse Core Ops, SparseCore 0:
  10.8 51.5 all-gather.18
  63.9 22.7 all-gather.20
  88.2 62.6 all-gather.16
  152.3 62.6 all-gather.22
  611.1 49.6 all-gather.18
  662.2 22.7 all-gather.20
  686.5 62.6 all-gather.16
  750.7 62.6 all-gather.22
Sparse Core Ops, SparseCore 1:
  1218.2 21.7 reduce-scatter.18
  1242.6 47.7 reduce-scatter.16
  1293.1 60.0 reduce-scatter.20
  1356.0 60.0 reduce-scatter.22
  1418.3 9.5 reduce-scatter.28
  1430.1 11.3 reduce-scatter.30
  1443.6 10.9 reduce-scatter.26
  1456.7 10.9 reduce-scatter.24
  1471.6 151.0 all-reduce.6
where the time goes:
time: 1650 us; the launch traced here: 1640 us
  matrix products  823 us (50%)
  waiting for transfers between devices  412 us (25%)
  other arithmetic  171 us (10%)
  blocking collectives  107 us (6%)
  local copies, waits for them, and re-layouts  104 us (6%)
  between operations  17.5 us (1%)
    dot_general x4, matrix products, attend_back(): jnp.einsum('hqk,qhd->khd', grad_scores, query_block, preferred_element_ty...  223 us
    dot_general x4, matrix products, attend_back(): jnp.einsum('hqk,khd->qhd', grad_scores, keys_low, preferred_element_type=...  208 us
    psum x1, waiting for transfers between devices, on_device(): lax.psum(s_qkv.astype(jnp.bfloat16), 'dp').astype(jnp.float32)  90.9 us
    all_gather x2, waiting for transfers between devices, micro_step(): lax.all_gather(w_out, 'fsdp', axis=0, tiled=True)  64.8 us
    reduce_scatter x1, waiting for transfers between devices, on_device(): lax.psum_scatter(g_wout.astype(jnp.bfloat16), 'fsdp', scatter_dimension=0...  62.9 us
    reduce_scatter x1, waiting for transfers between devices, on_device(): lax.psum_scatter(g_win.astype(jnp.bfloat16), 'fsdp', scatter_dimension=0,...  62.8 us
    psum x1, blocking collectives, on_device(): lax.psum(s_gain.astype(jnp.bfloat16), 'dp').astype(jnp.float32)  59.5 us
    dot_general x4, matrix products, attend(): jnp.einsum('hqk,khd->qhd', probs.astype(jnp.bfloat16), values_low, prefer...  50.1 us
  transfers between devices with their start and end apart: 17, of which 12 were waited for; matrix products, arithmetic and copies ran while one was open for 17% of the time, Pallas kernels for 0%

commit v1 on v0

v1 whole, which is shorter than its diff:
```python
import functools
import math

import jax
import jax.numpy as jnp
from jax import lax
from jax.experimental import pallas as pl
from jax.experimental.pallas import tpu as pltpu
from jax.sharding import PartitionSpec as P

H = 12
HD = 64
PAIR = 2 * HD
GROUP = 3
BLK = 256
MASK = 256.0
LOG2E = math.log2(math.e)
f32 = jnp.float32
bf16 = jnp.bfloat16
NT = (((1,), (1,)), ((), ()))


def dot(a, b):
    return jnp.dot(a, b, preferred_element_type=f32)


def dot_nt(a, b):
    return lax.dot_general(a, b, NT, preferred_element_type=f32)


def lanes(rows):
    return lax.broadcasted_iota(jnp.int32, (rows, PAIR), 1)


def half_matrix(same, value):
    i = lax.broadcasted_iota(jnp.int32, (PAIR, PAIR), 0) // HD
    j = lax.broadcasted_iota(jnp.int32, (PAIR, PAIR), 1) // HD
    hit = (i == j) if same else (i != j)
    return jnp.where(hit, value, 0.0).astype(bf16)


def head_stats(raw, averager):
    mean = dot(raw, averager)
    centered = raw.astype(f32) - mean
    variance = dot((centered * centered).astype(bf16), averager)
    rstd = lax.rsqrt(variance + 1e-6)
    return centered * rstd, rstd


def split(v):
    high = v.astype(bf16)
    low = (v - high.astype(f32)).astype(bf16)
    return high, low


def query_extra(pic, lane):
    slot = lane % HD
    hot = jnp.where(slot == pic, MASK, 0.0)
    return jnp.where(slot == 11, -MASK, hot)


def key_extra(pic, lane):
    slot = lane % HD
    hot = jnp.where(slot == pic, 1.0, 0.0)
    return jnp.where(slot == 11, 1.0, jnp.where((slot == 12) | (slot == 13), -1.0, hot))


def forward_kernel(
    bounds, q_ref, k_ref, v_ref, pic_ref, gain_ref, out_ref, lse_ref, qa, ka, va, acc
):
    row = pl.program_id(0)
    slots = q_ref.shape[1]
    blocks = slots // BLK
    averager = half_matrix(True, 1.0 / HD)
    lane = lanes(BLK)
    low_half = lane < HD
    heads = 2 * GROUP

    def prepare(b, _):
        at = pl.ds(pl.multiple_of(b * BLK, BLK), BLK)
        pic = pic_ref[0, at, :]
        q_more = query_extra(pic, lane)
        k_more = key_extra(pic, lane)
        for p in range(GROUP):
            col = slice(p * PAIR, (p + 1) * PAIR)
            normed, _unused = head_stats(q_ref[0, at, col], averager)
            q = (normed * gain_ref[0:1, :]).astype(bf16).astype(f32) * 0.125
            normed, _unused = head_stats(k_ref[0, at, col], averager)
            k = normed * gain_ref[1:2, :]
            v = v_ref[0, at, col].astype(f32)
            qa[2 * p, at, :] = jnp.where(low_half, q, q_more).astype(bf16)
            qa[2 * p + 1, at, :] = jnp.where(low_half, q_more, q).astype(bf16)
            ka[2 * p, at, :] = jnp.where(low_half, k, k_more).astype(bf16)
            ka[2 * p + 1, at, :] = jnp.where(low_half, k_more, k).astype(bf16)
            va[2 * p, at, :] = jnp.where(low_half, v, 1.0).astype(bf16)
            va[2 * p + 1, at, :] = jnp.where(low_half, 1.0, v).astype(bf16)
        return 0

    lax.fori_loop(0, blocks, prepare, 0)

    def query_block(b, _):
        at = pl.ds(pl.multiple_of(b * BLK, BLK), BLK)
        acc[...] = jnp.zeros_like(acc)

        def key_block(kb, _):
            keys = pl.ds(pl.multiple_of(kb * BLK, BLK), BLK)
            for h in range(heads):
                scores = dot_nt(qa[h, at, :], ka[h, keys, :])
                probs = jnp.exp2(scores * LOG2E).astype(bf16)
                acc[h] += dot(probs, va[h, keys, :])
            return 0

        lax.fori_loop(bounds[row, 0, b], bounds[row, 1, b], key_block, 0)
        for p in range(GROUP):
            col = slice(p * PAIR, (p + 1) * PAIR)
            even, odd = acc[2 * p], acc[2 * p + 1]
            crossed = jnp.where(low_half, odd, even)
            total = pltpu.roll(crossed, HD, 1)
            out_ref[0, at, col] = (jnp.where(low_half, even, odd) / total).astype(bf16)
            lse_ref[0, at, col] = jnp.log(crossed)
        return 0

    lax.fori_loop(0, blocks, query_block, 0)


def backward_kernel(
    bounds,
    q_ref,
    k_ref,
    v_ref,
    o_ref,
    g_ref,
    lse_ref,
    pic_ref,
    gain_ref,
    out_ref,
    stat_ref,
    qa,
    ka,
    va,
    ga,
    kt,
    dqt,
    dk,
    dv,
):
    row = pl.program_id(0)
    slots = q_ref.shape[1]
    blocks = slots // BLK
    averager = half_matrix(True, 1.0 / HD)
    crosser = half_matrix(False, 1.0)
    lane = lanes(BLK)
    slot = lane % HD
    low_half = lane < HD
    heads = 2 * GROUP

    def prepare(b, _):
        at = pl.ds(pl.multiple_of(b * BLK, BLK), BLK)
        pic = pic_ref[0, at, :]
        q_hot = query_extra(pic, lane)
        k_more = key_extra(pic, lane)
        for p in range(GROUP):
            col = slice(p * PAIR, (p + 1) * PAIR)
            lse = lse_ref[0, at, col]
            lse_high = lse.astype(bf16).astype(f32)
            q_more = jnp.where(slot == 12, lse_high, jnp.where(slot == 13, lse - lse_high, q_hot))
            normed, _unused = head_stats(q_ref[0, at, col], averager)
            q = (normed * gain_ref[0:1, :]).astype(bf16).astype(f32) * 0.125
            normed, _unused = head_stats(k_ref[0, at, col], averager)
            k = normed * gain_ref[1:2, :]
            v = v_ref[0, at, col].astype(f32)
            g = g_ref[0, at, col].astype(f32)
            high, low = split(g * o_ref[0, at, col].astype(f32))
            centre = dot(high, crosser) + dot(low, crosser)
            centre_high = centre.astype(bf16).astype(f32)
            g_more = jnp.where(
                slot == 12, centre_high, jnp.where(slot == 13, centre - centre_high, 0.0)
            )
            v_more = jnp.where((slot == 12) | (slot == 13), -1.0, 0.0)
            qa[2 * p, at, :] = jnp.where(low_half, q, q_more).astype(bf16)
            qa[2 * p + 1, at, :] = jnp.where(low_half, q_more, q).astype(bf16)
            ka[2 * p, at, :] = jnp.where(low_half, k, k_more).astype(bf16)
            ka[2 * p + 1, at, :] = jnp.where(low_half, k_more, k).astype(bf16)
            va[2 * p, at, :] = jnp.where(low_half, v, v_more).astype(bf16)
            va[2 * p + 1, at, :] = jnp.where(low_half, v_more, v).astype(bf16)
            ga[2 * p, at, :] = jnp.where(low_half, g, g_more).astype(bf16)
            ga[2 * p + 1, at, :] = jnp.where(low_half, g_more, g).astype(bf16)
            kt[p, :, at] = k.astype(bf16).T
        return 0

    lax.fori_loop(0, blocks, prepare, 0)
    dqt[...] = jnp.zeros_like(dqt)
    stat_ref[...] = jnp.zeros_like(stat_ref)

    def pull_norm(raw, grad, gain):
        normed, rstd = head_stats(raw, averager)
        lifted = grad * gain
        mean_one = dot(lifted.astype(bf16), averager)
        mean_two = dot((lifted * normed).astype(bf16), averager)
        raw_grad = rstd * (lifted - mean_one - normed * mean_two)
        return raw_grad.astype(bf16), jnp.sum(grad * normed, axis=0, keepdims=True)

    def key_block(b, _):
        keys = pl.ds(pl.multiple_of(b * BLK, BLK), BLK)
        dk[...] = jnp.zeros_like(dk)
        dv[...] = jnp.zeros_like(dv)

        def query_block(qb, _):
            at = pl.ds(pl.multiple_of(qb * BLK, BLK), BLK)
            for h in range(heads):
                p, half = h // 2, slice((h % 2) * HD, (h % 2 + 1) * HD)
                scores = dot_nt(ka[h, keys, :], qa[h, at, :])
                probs = jnp.exp2(scores * LOG2E)
                pulls = dot_nt(va[h, keys, :], ga[h, at, :])
                grads = (probs * pulls).astype(bf16)
                dv[h] += dot(probs.astype(bf16), ga[h, at, :])
                dk[h] += dot(grads, qa[h, at, :])
                dqt[p, half, at] += dot(kt[p, half, keys], grads)
            return 0

        lax.fori_loop(bounds[row, 2, b], bounds[row, 3, b], query_block, 0)
        for p in range(GROUP):
            col = slice(p * PAIR, (p + 1) * PAIR)
            grad = jnp.where(low_half, dk[2 * p], dk[2 * p + 1])
            raw_grad, gain_grad = pull_norm(k_ref[0, keys, col], grad, gain_ref[1:2, :])
            out_ref[1, 0, keys, col] = raw_grad
            stat_ref[0, 1:2, col] += gain_grad
            stat_ref[0, 3:4, col] += jnp.sum(raw_grad.astype(f32), axis=0, keepdims=True)
            grad_v = jnp.where(low_half, dv[2 * p], dv[2 * p + 1]).astype(bf16)
            out_ref[2, 0, keys, col] = grad_v
            stat_ref[0, 4:5, col] += jnp.sum(grad_v.astype(f32), axis=0, keepdims=True)
        return 0

    lax.fori_loop(0, blocks, key_block, 0)

    def finish(b, _):
        at = pl.ds(pl.multiple_of(b * BLK, BLK), BLK)
        for p in range(GROUP):
            col = slice(p * PAIR, (p + 1) * PAIR)
            grad = dqt[p, :, at].T * 0.125
            raw_grad, gain_grad = pull_norm(q_ref[0, at, col], grad, gain_ref[0:1, :])
            out_ref[0, 0, at, col] = raw_grad
            stat_ref[0, 0:1, col] += gain_grad
            stat_ref[0, 2:3, col] += jnp.sum(raw_grad.astype(f32), axis=0, keepdims=True)
        return 0

    lax.fori_loop(0, blocks, finish, 0)


def attention(qkv, pic, bounds, gains):
    rows, slots, _ = qkv.shape
    width = qkv.shape[2] // 3
    wide = GROUP * PAIR
    groups = width // wide
    flops = rows * H * slots * slots * 256 * 4
    part = lambda i: pl.BlockSpec((1, slots, wide), lambda r, g, b: (r, 0, i * groups + g))
    whole = pl.BlockSpec((1, slots, wide), lambda r, g, b: (r, 0, g))
    return pl.pallas_call(
        forward_kernel,
        name="attention_forward",
        grid_spec=pltpu.PrefetchScalarGridSpec(
            num_scalar_prefetch=1,
            grid=(rows, groups),
            in_specs=[
                part(0),
                part(1),
                part(2),
                pl.BlockSpec((1, slots, 1), lambda r, g, b: (r, 0, 0)),
                pl.BlockSpec((2, PAIR), lambda r, g, b: (0, 0)),
            ],
            out_specs=[whole, whole],
            scratch_shapes=[
                pltpu.VMEM((2 * GROUP, slots, PAIR), bf16),
                pltpu.VMEM((2 * GROUP, slots, PAIR), bf16),
                pltpu.VMEM((2 * GROUP, slots, PAIR), bf16),
                pltpu.VMEM((2 * GROUP, BLK, PAIR), f32),
            ],
        ),
        out_shape=[
            jax.ShapeDtypeStruct((rows, slots, width), bf16),
            jax.ShapeDtypeStruct((rows, slots, width), f32),
        ],
        cost_estimate=pl.CostEstimate(
            flops=flops, bytes_accessed=rows * slots * width * 12, transcendentals=0
        ),
        compiler_params=pltpu.CompilerParams(vmem_limit_bytes=48 << 20),
    )(bounds, qkv, qkv, qkv, pic, gains)


def attention_back(qkv, attn, grad_attn, lse, pic, bounds, gains):
    rows, slots, _ = qkv.shape
    width = qkv.shape[2] // 3
    wide = GROUP * PAIR
    groups = width // wide
    flops = rows * H * slots * slots * 256 * 10
    part = lambda i: pl.BlockSpec((1, slots, wide), lambda r, g, b: (r, 0, i * groups + g))
    whole = pl.BlockSpec((1, slots, wide), lambda r, g, b: (r, 0, g))
    return pl.pallas_call(
        backward_kernel,
        name="attention_backward",
        grid_spec=pltpu.PrefetchScalarGridSpec(
            num_scalar_prefetch=1,
            grid=(rows, groups),
            in_specs=[
                part(0),
                part(1),
                part(2),
                whole,
                whole,
                whole,
                pl.BlockSpec((1, slots, 1), lambda r, g, b: (r, 0, 0)),
                pl.BlockSpec((2, PAIR), lambda r, g, b: (0, 0)),
            ],
            out_specs=[
                pl.BlockSpec((3, 1, slots, wide), lambda r, g, b: (0, r, 0, g)),
                pl.BlockSpec((1, 8, wide), lambda r, g, b: (r, 0, g)),
            ],
            scratch_shapes=[
                pltpu.VMEM((2 * GROUP, slots, PAIR), bf16),
                pltpu.VMEM((2 * GROUP, slots, PAIR), bf16),
                pltpu.VMEM((2 * GROUP, slots, PAIR), bf16),
                pltpu.VMEM((2 * GROUP, slots, PAIR), bf16),
                pltpu.VMEM((GROUP, PAIR, slots), bf16),
                pltpu.VMEM((GROUP, PAIR, slots), f32),
                pltpu.VMEM((2 * GROUP, BLK, PAIR), f32),
                pltpu.VMEM((2 * GROUP, BLK, PAIR), f32),
            ],
        ),
        out_shape=[
            jax.ShapeDtypeStruct((3, rows, slots, width), bf16),
            jax.ShapeDtypeStruct((rows, 8, width), f32),
        ],
        cost_estimate=pl.CostEstimate(
            flops=flops, bytes_accessed=rows * slots * width * 20, transcendentals=0
        ),
        compiler_params=pltpu.CompilerParams(vmem_limit_bytes=56 << 20),
    )(bounds, qkv, qkv, qkv, attn, grad_attn, lse, pic, gains)


def picture_tables(lengths, slots):
    ends = jnp.cumsum(lengths, axis=1)
    position = jnp.arange(slots, dtype=jnp.int32)
    pic = jnp.sum((position[None, :, None] >= ends[:, None, :]).astype(jnp.int32), axis=2)
    inside = (position[None, :] < ends[:, -1:]).astype(f32)
    first = jnp.arange(0, slots, BLK, dtype=jnp.int32)
    last = first + (BLK - 1)
    before = jnp.where(ends[:, None, :] <= first[None, :, None], ends[:, None, :], 0)
    begin = jnp.max(before, axis=2)
    after = jnp.where(ends[:, None, :] > last[None, :, None], ends[:, None, :], slots)
    end = jnp.min(after, axis=2)
    low = begin // BLK
    high = (end + BLK - 1) // BLK
    used = ((ends[:, -1:] + BLK - 1) // BLK) * jnp.ones_like(high)
    index = jnp.arange(slots // BLK, dtype=jnp.int32)[None, :]
    low_back = low
    high_back = jnp.where(index < used, jnp.minimum(high, used), low)
    bounds = jnp.stack([low, high, low_back, high_back], axis=1).astype(jnp.int32)
    return pic.astype(jnp.int32), inside, bounds


def norm_stats(values):
    mean = jnp.mean(values, axis=-1, keepdims=True)
    centered = values - mean
    variance = jnp.mean(centered * centered, axis=-1, keepdims=True)
    rstd = lax.rsqrt(variance + 1e-6)
    return centered * rstd, rstd


def norm_back(grad, normed, rstd, gain):
    lifted = grad * gain
    mean_one = jnp.mean(lifted, axis=-1, keepdims=True)
    mean_two = jnp.mean(lifted * normed, axis=-1, keepdims=True)
    return (
        rstd * (lifted - mean_one - normed * mean_two),
        jnp.sum(grad * normed, axis=0),
        jnp.sum(grad, axis=0),
    )


class Place:
    def __init__(self, fsdp, replicas):
        self.groups, self.rests = fsdp, replicas // 4
        dp = lax.axis_index("dp")
        self.f = lax.axis_index("fsdp")
        self.core = lax.rem(dp, 2)
        self.side = lax.rem(dp // 2, 2)
        self.rest = dp // 4

    def device(self, f=None, core=None, side=None, rest=None):
        f = self.f if f is None else f
        core = self.core if core is None else core
        side = self.side if side is None else side
        rest = self.rest if rest is None else rest
        return ((rest * 2 + side) * 2 + core, f)


def remote(src, dst, send, recv, device):
    return pltpu.make_async_remote_copy(
        src_ref=src,
        dst_ref=dst,
        send_sem=send,
        recv_sem=recv,
        device_id=device,
        device_id_type=pl.DeviceIdType.MESH,
    )


def greet(devices):
    barrier = pltpu.get_barrier_semaphore()
    for device in devices:
        pl.semaphore_signal(
            barrier, inc=1, device_id=device, device_id_type=pl.DeviceIdType.MESH
        )
    pl.semaphore_wait(barrier, len(devices))


def gather_kernel(fsdp, replicas, pieces, *refs):
    count = len(pieces)
    shards, fulls = refs[:count], refs[count : 2 * count]
    own_sem, out_send, out_recv, side_send, side_recv = refs[2 * count :]
    me = Place(fsdp, replicas)
    sibling = me.device(core=1 - me.core)
    peers = [lax.rem(me.f + k, fsdp) for k in range(1, fsdp)]
    sources = [lax.rem(me.f + fsdp - k, fsdp) for k in range(1, fsdp)]
    greet([sibling] + [me.device(f=peer) for peer in peers])
    own, outer, inner = [], [], []
    for i in range(count):
        for start, size in pieces[i]:
            col = pl.ds(start, size)
            for k, peer in enumerate(peers):
                at = len(outer)
                copy = remote(
                    shards[i].at[me.core, :, col],
                    fulls[i].at[me.f, me.core, :, col],
                    out_send.at[at],
                    out_recv.at[at],
                    me.device(f=peer),
                )
                copy.start()
                outer.append((copy, i, col, k))
    for i in range(count):
        copy = pltpu.make_async_copy(shards[i], fulls[i].at[me.f], own_sem.at[i])
        copy.start()
        own.append(copy)
    for at, (copy, i, col, k) in enumerate(outer):
        copy.wait_recv()
        landed = fulls[i].at[sources[k], me.core, :, col]
        forward = remote(landed, landed, side_send.at[at], side_recv.at[at], sibling)
        forward.start()
        inner.append(forward)
    for copy, *_ in outer:
        copy.wait_send()
    for copy in inner:
        copy.wait()
    for copy in own:
        copy.wait()


def gather_halves(fsdp, replicas, shards, pieces):
    copies = sum(len(item) for item in pieces) * (fsdp - 1)
    any_space = pl.BlockSpec(memory_space=pl.ANY)
    return pl.pallas_call(
        functools.partial(gather_kernel, fsdp, replicas, pieces),
        name="gather_halves",
        in_specs=[any_space] * len(shards),
        out_specs=[any_space] * len(shards),
        out_shape=[jax.ShapeDtypeStruct((fsdp,) + item.shape, item.dtype) for item in shards],
        scratch_shapes=[pltpu.SemaphoreType.DMA((len(shards),))]
        + [pltpu.SemaphoreType.DMA((copies,))] * 4,
        compiler_params=pltpu.CompilerParams(collective_id=1, has_side_effects=True),
    )(*shards)


def add_into(dst, sources):
    def step(i, _):
        total = sources[0][i].astype(f32)
        for item in sources[1:]:
            total = total + item[i].astype(f32)
        dst[i] = total.astype(bf16)
        return 0

    lax.fori_loop(0, dst.shape[0], step, 0)


def reduce_kernel(fsdp, replicas, count, *refs):
    grads, outs = refs[:count], refs[count : 2 * count]
    from_core = refs[2 * count : 3 * count]
    from_group = refs[3 * count : 4 * count]
    from_side = refs[4 * count : 5 * count]
    from_rest = refs[5 * count : 6 * count]
    send, recv = refs[6 * count :]
    me = Place(fsdp, replicas)
    rests = replicas // 4
    sibling = me.device(core=1 - me.core)
    across = me.device(side=1 - me.side)
    groups = [lax.rem(me.f + k, fsdp) for k in range(1, fsdp)]
    others = [lax.rem(me.rest + k, rests) for k in range(1, rests)]
    greet(
        [sibling, across]
        + [me.device(f=item) for item in groups]
        + [me.device(rest=item) for item in others]
    )
    used = [0]

    def start(src, dst, device):
        at = used[0]
        used[0] += 1
        copy = remote(src, dst, send.at[at], recv.at[at], device)
        copy.start()
        return copy

    sent = []
    flying = [None] * count

    def stage(i, number):
        if number > 0:
            for copy in flying[i]:
                copy.wait_recv()
                sent.append(copy)
        begun = []
        if number == 0:
            for f in range(fsdp):
                begun.append(
                    start(grads[i].at[f, :, :, 1 - me.core], from_core[i].at[f], sibling)
                )
        elif number == 1:
            for f in range(fsdp):
                for side in range(2):
                    add_into(
                        from_core[i].at[f, :, side],
                        [grads[i].at[f, :, side, me.core], from_core[i].at[f, :, side]],
                    )
            for k, f in enumerate(groups):
                begun.append(start(from_core[i].at[f], from_group[i].at[k], me.device(f=f)))
        elif number == 2:
            for side in range(2):
                add_into(
                    from_group[i].at[0, :, side],
                    [from_core[i].at[me.f, :, side]]
                    + [from_group[i].at[k, :, side] for k in range(fsdp - 1)],
                )
            begun.append(start(from_group[i].at[0, :, 1 - me.side], from_side[i], across))
        elif number == 3:
            add_into(from_side[i], [from_group[i].at[0, :, me.side], from_side[i]])
            for k, rest in enumerate(others):
                begun.append(
                    start(from_side[i].at[rest], from_rest[i].at[k], me.device(rest=rest))
                )
        elif number == 4:
            mine = outs[i].at[pl.ds(me.rest, 1), me.side, me.core]
            add_into(
                mine,
                [from_side[i].at[pl.ds(me.rest, 1)]]
                + [from_rest[i].at[pl.ds(k, 1)] for k in range(rests - 1)],
            )
            for rest in others:
                begun.append(start(mine, mine, me.device(rest=rest)))
        elif number == 5:
            mine = outs[i].at[:, me.side, me.core]
            begun.append(start(mine, mine, across))
        elif number == 6:
            mine = outs[i].at[:, :, me.core]
            begun.append(start(mine, mine, sibling))
        flying[i] = begun

    stages = 8
    for tick in range(stages + count - 1):
        for i in range(count):
            number = tick - i
            if 0 <= number < stages:
                stage(i, number)
    for copy in sent:
        copy.wait_send()


def reduce_everywhere(fsdp, replicas, grads):
    rests = replicas // 4
    count = len(grads)
    tails = [item.shape[-2:] for item in grads]
    copies = count * (fsdp + (fsdp - 1) + 1 + (rests - 1) + (rests - 1) + 2)
    vmem = pl.BlockSpec(memory_space=pltpu.VMEM)
    return pl.pallas_call(
        functools.partial(reduce_kernel, fsdp, replicas, count),
        name="reduce_everywhere",
        in_specs=[vmem] * count,
        out_specs=[vmem] * count,
        out_shape=[jax.ShapeDtypeStruct((rests, 2, 2) + tail, bf16) for tail in tails],
        scratch_shapes=[pltpu.VMEM((fsdp, rests, 2) + tail, bf16) for tail in tails]
        + [pltpu.VMEM((fsdp - 1, rests, 2) + tail, bf16) for tail in tails]
        + [pltpu.VMEM((rests,) + tail, bf16) for tail in tails]
        + [pltpu.VMEM((rests - 1,) + tail, bf16) for tail in tails]
        + [pltpu.SemaphoreType.DMA((copies,))] * 2,
        compiler_params=pltpu.CompilerParams(
            collective_id=2, has_side_effects=True, vmem_limit_bytes=60 << 20
        ),
    )(*grads)


GELU_C = math.sqrt(2.0 / math.pi)


def gelu_both(v):
    square = v * v
    t = jnp.tanh(GELU_C * v * (1.0 + 0.044715 * square))
    half = 0.5 * (1.0 + t)
    slope = half + 0.5 * v * (1.0 - t * t) * GELU_C * (1.0 + 3 * 0.044715 * square)
    return v * half, slope


def on_device(fsdp, replicas, *args):
    (
        patches,
        ln_gain,
        ln_bias,
        w_qkv,
        b_qkv,
        qk_gain,
        w_proj,
        out_bias,
        w_in,
        b_in,
        w_out,
        lengths,
        cotangent,
    ) = args
    rows, slots, width = patches.shape
    tokens = rows * slots
    small = (ln_gain, ln_bias, b_qkv, qk_gain, out_bias, b_in)
    flat = jnp.concatenate([item.reshape(-1) for item in small])
    small_cols = -(-flat.shape[0] // (32 * PAIR)) * PAIR
    flat = jnp.pad(flat, (0, 32 * small_cols - flat.shape[0])).reshape(2, 16, small_cols)
    shard_rows, columns = w_qkv.shape
    third = columns // 3
    w_qkv_full, flat_full = gather_halves(
        fsdp,
        replicas,
        [w_qkv.reshape(2, shard_rows // 2, columns), flat],
        [[(0, third), (third, third), (2 * third, third)], [(0, small_cols)]],
    )
    w_qkv_full = w_qkv_full.reshape(width, columns)
    flat_full, w_proj, w_in, w_out = lax.optimization_barrier((flat_full, w_proj, w_in, w_out))
    flat_full = flat_full.reshape(fsdp, -1).astype(f32)
    full_small = []
    at = 0
    for item in small:
        size = item.size
        piece = flat_full[:, at : at + size].reshape((fsdp,) + item.shape)
        at += size
        full_small.append(jnp.moveaxis(piece, 0, -2).reshape(item.shape[:-1] + (-1,)))
    gains, shifts, b_qkv_full, qk_gain_full, out_bias_full, b_in_full = full_small
    w_proj_full = lax.all_gather(w_proj, "fsdp", axis=0, tiled=True)
    w_in_full = lax.all_gather(w_in, "fsdp", axis=0, tiled=True)
    w_out_full = lax.all_gather(w_out, "fsdp", axis=0, tiled=True)

    pic, inside, bounds = picture_tables(lengths, slots)
    pic = pic[:, :, None]
    pair_gain = jnp.concatenate([qk_gain_full, qk_gain_full], axis=1)
    inside = inside.reshape(tokens, 1)

    source = patches.reshape(tokens, width).astype(f32)
    n1, rstd1 = norm_stats(source)
    normed1 = (n1 * gains[0] + shifts[0]).astype(bf16)
    qkv = (dot(normed1, w_qkv_full) + b_qkv_full).astype(bf16).reshape(rows, slots, columns)
    attn, lse = attention(qkv, pic, bounds, pair_gain)
    attn_flat = attn.reshape(tokens, width)
    resid = source + dot(attn_flat, w_proj_full) + out_bias_full[0]
    n2, rstd2 = norm_stats(resid)
    normed2 = (n2 * gains[1] + shifts[1]).astype(bf16)
    grad_y = cotangent.reshape(tokens, width).astype(f32) * inside
    grad_mlp = grad_y.astype(bf16)

    hidden = dot(normed2, w_in_full) + b_in_full
    activated, slope = gelu_both(hidden)
    activated = activated.astype(bf16)
    block_out = resid + dot(activated, w_out_full) + out_bias_full[1]
    block_out = block_out.astype(bf16)
    grad_hidden = (dot_nt(grad_mlp, w_out_full) * slope).astype(bf16)
    tt = (((0,), (0,)), ((), ()))
    grad_w_out = lax.dot_general(activated, grad_mlp, tt, preferred_element_type=f32).astype(bf16)
    grad_w_in = lax.dot_general(normed2, grad_hidden, tt, preferred_element_type=f32).astype(bf16)
    grad_b_in = jnp.sum(grad_hidden.astype(f32), axis=0)
    grad_bias_mlp = jnp.sum(grad_y, axis=0)
    grad_norm2 = dot_nt(grad_hidden, w_in_full)
    back2, grad_gain2, grad_shift2 = norm_back(grad_norm2, n2, rstd2, gains[1])
    grad_resid = grad_y + back2
    grad_branch = grad_resid.astype(bf16)
    grad_bias_attn = jnp.sum(grad_branch.astype(f32), axis=0)
    grad_attn = dot_nt(grad_branch, w_proj_full).astype(bf16)
    grad_w_proj = lax.dot_general(attn_flat, grad_branch, tt, preferred_element_type=f32).astype(bf16)

    grad_qkv, stats = attention_back(
        qkv, attn, grad_attn.reshape(rows, slots, width), lse, pic, bounds, pair_gain
    )
    stats = jnp.sum(stats, axis=0)
    grad_qk_gain = jnp.sum(stats[0:2].reshape(2, H, HD), axis=1)
    grad_b_qkv = stats[2:5].reshape(-1)
    grad_qkv = grad_qkv.reshape(3, tokens, width)
    grad_w_qkv = [
        lax.dot_general(normed1, grad_qkv[i], tt, preferred_element_type=f32).astype(bf16)
        for i in range(3)
    ]
    grad_norm1 = sum(
        dot_nt(grad_qkv[i], w_qkv_full[:, i * width : (i + 1) * width]) for i in range(3)
    )
    back1, grad_gain1, grad_shift1 = norm_back(grad_norm1, n1, rstd1, gains[0])
    grad_patches = (grad_resid + back1).reshape(rows, slots, width)

    small_grads = (
        jnp.stack([grad_gain1, grad_gain2]),
        jnp.stack([grad_shift1, grad_shift2]),
        grad_b_qkv,
        grad_qk_gain,
        jnp.stack([grad_bias_attn, grad_bias_mlp]),
        grad_b_in,
    )
    flat_grads = jnp.concatenate(
        [
            jnp.moveaxis(item.reshape(item.shape[:-1] + (fsdp, -1)), -2, 0).reshape(fsdp, -1)
            for item in small_grads
        ],
        axis=1,
    ).astype(bf16)
    lead = (fsdp, replicas // 4, 2, 2)
    hidden_blocks = w_in.shape[1] // width
    small_rows = 16
    flat_grads = jnp.pad(
        flat_grads, ((0, 0), (0, replicas * small_rows * width - flat_grads.shape[1]))
    )
    qkv_rows = jnp.stack(grad_w_qkv).reshape(3, fsdp, shard_rows, width)
    qkv_rows = jnp.swapaxes(qkv_rows, 0, 1).reshape(lead + (-1, width))
    proj_rows = grad_w_proj.reshape(lead + (-1, width))
    last_rows = [proj_rows, qkv_rows, flat_grads.reshape(lead + (small_rows, width))]
    last_sizes = [item.shape[-2] for item in last_rows]
    spare = -sum(last_sizes) % 16
    last_rows.append(jnp.zeros(lead + (spare, width), bf16))
    in_rows = grad_w_in.reshape(fsdp, shard_rows, hidden_blocks, width)
    in_rows = jnp.moveaxis(in_rows, 2, 1).reshape(lead + (-1, width))
    out_rows = grad_w_out.reshape(lead + (-1, width))
    r_out, r_in, r_last = reduce_everywhere(
        fsdp, replicas, [out_rows, in_rows, jnp.concatenate(last_rows, axis=-2)]
    )
    r_w_out = r_out.reshape(-1, width)
    r_w_in = jnp.moveaxis(r_in.reshape(hidden_blocks, shard_rows, width), 0, 1)
    r_w_in = r_w_in.reshape(shard_rows, -1)
    first, second = last_sizes[0], last_sizes[0] + last_sizes[1]
    r_w_proj = r_last[..., :first, :].reshape(-1, width)
    r_w_qkv = r_last[..., first:second, :].reshape(3, shard_rows, width)
    r_w_qkv = jnp.swapaxes(r_w_qkv, 0, 1).reshape(shard_rows, columns)
    r_flat = r_last[..., second : second + small_rows, :].reshape(-1).astype(f32)
    r_small = []
    at = 0
    for item in small:
        r_small.append(r_flat[at : at + item.size].reshape(item.shape))
        at += item.size
    return (
        block_out.reshape(rows, slots, width),
        grad_patches,
        r_small[0],
        r_small[1],
        r_w_qkv.astype(f32),
        r_small[2],
        r_small[3],
        r_w_proj.astype(f32),
        r_small[4],
        r_w_in.astype(f32),
        r_small[5],
        r_w_out.astype(f32),
    )


def solution(mesh):
    fsdp = mesh.shape["fsdp"]
    replicas = mesh.shape["dp"]
    every = ("dp", "fsdp")
    by_row = P(every, None, None)
    last, lead = P(None, "fsdp"), P("fsdp", None)
    placed = (
        by_row,
        last,
        last,
        lead,
        P("fsdp"),
        last,
        lead,
        last,
        lead,
        P("fsdp"),
        lead,
        P(every, None),
        by_row,
    )
    outs = (by_row, by_row, last, last, lead, P("fsdp"), last, lead, last, lead, P("fsdp"), lead)
    return jax.shard_map(
        functools.partial(on_device, fsdp, replicas),
        mesh=mesh,
        in_specs=placed,
        out_specs=outs,
        check_vma=False,
    )
```

time: 1650 us -> 759 us (0.46)
  matrix products: 823 us -> 186 us
  Pallas kernels: 0 us -> 429 us
  waiting for transfers between devices: 412 us -> 18.4 us
  other arithmetic: 171 us -> 39.6 us
  blocking collectives: 107 us -> 0 us
  local copies, waits for them, and re-layouts: 104 us -> 64.6 us
    dot_general x48 -> x16, matrix products: 823 us -> 186 us  [the longest x6 68.1 us: dot_nt(): return lax.dot_general(a, b, NT, preferred_element_type=f32)]
    pallas_call x0 -> x4, Pallas kernels: none -> 429 us  [the longest x1 198 us: reduce_everywhere(): pl.pallas_call(functools.partial(reduce_kernel, fsdp, replicas, count), n...]
    reduce_scatter x4 -> x0, waiting for transfers between devices: 175 us -> none  [the longest x1 62.9 us: on_device(): lax.psum_scatter(g_wout.astype(jnp.bfloat16), 'fsdp', scatter_dimension=0...]
    psum x1 -> x0, waiting for transfers between devices: 90.9 us -> none  [on_device(): lax.psum(s_qkv.astype(jnp.bfloat16), 'dp').astype(jnp.float32)]
    reduce_sum x32 -> x8, other arithmetic: 98.7 us -> 9.37 us  [the longest x1 5.34 us: on_device(): grad_bias_attn = jnp.sum(grad_branch.astype(f32), axis=0)]
    all_gather x8 -> x3, waiting for transfers between devices: 99.8 us -> 17 us  [the longest x1 17 us: on_device(): w_out_full = lax.all_gather(w_out, 'fsdp', axis=0, tiled=True)]
    psum x1 -> x0, blocking collectives: 59.5 us -> none  [on_device(): lax.psum(s_gain.astype(jnp.bfloat16), 'dp').astype(jnp.float32)]
    all_gather x12 -> x0, blocking collectives: 41.9 us -> none  [the longest x2 7.63 us: micro_step(): lax.all_gather(b_in, 'fsdp', axis=0, tiled=True)]
  transfers between devices with their start and end apart: 17 -> 3, of which waited for: 12 -> 1; matrix products, arithmetic and copies ran while one was open for 17% -> 10% of each run, Pallas kernels for 0% -> 8%
where the time goes in v1:
time: 759 us; the launch traced here: 753 us
  Pallas kernels  429 us (57%)
  matrix products  186 us (25%)
  local copies, waits for them, and re-layouts  64.6 us (9%)
  other arithmetic  39.6 us (5%)
  waiting for transfers between devices  18.4 us (2%)
  between operations  14.8 us (2%)
    pallas_call x1, Pallas kernels, reduce_everywhere(): pl.pallas_call(functools.partial(reduce_kernel, fsdp, replicas, count), n...  198 us
    pallas_call x1, Pallas kernels, attention_back(): pl.pallas_call(backward_kernel, name='attention_backward', grid_spec=pltp...  117 us
    dot_general x6, matrix products, dot_nt(): return lax.dot_general(a, b, NT, preferred_element_type=f32)  68.1 us
    dot_general x4, matrix products, dot(): return jnp.dot(a, b, preferred_element_type=f32)  58.8 us
    pallas_call x1, Pallas kernels, gather_halves(): pl.pallas_call(functools.partial(gather_kernel, fsdp, replicas, pieces),...  57.4 us
    pallas_call x1, Pallas kernels, attention(): pl.pallas_call(forward_kernel, name='attention_forward', grid_spec=pltpu....  56.5 us
    dot_general x1, matrix products, on_device(): lax.dot_general(activated, grad_mlp, tt, preferred_element_type=f32)  21.3 us
    dot_general x1, matrix products, on_device(): lax.dot_general(normed2, grad_hidden, tt, preferred_element_type=f32)  19.9 us
  transfers between devices with their start and end apart: 3, of which 1 were waited for; matrix products, arithmetic and copies ran while one was open for 10% of the time, Pallas kernels for 8%

profile of v1, /device:TPU:1, one launch (start us, length us, event | category | flops | bytes accessed | tf_op | source)
XLA Modules:
  0.0 753.0 jit_solution(4244660465268510711)
XLA Ops:
  12.3 57.4 %gather_halves.1 = (bf16[2,2,192,2304]{3,2,1,0:T(8,128)(2,1)}, bf16[2,2,16,256]{3,2,1,0:T(8,128)(2,1)}) custom-call(bf16[2,192,2304]{2,1,0:T(8,128)(2,1)} %bitcast.179, bf16[2,16,256]{2,1,0:T(8,128)(2,1)} %reshape.572.refs_1_), custom_call_target="tpu_custom_call" | custom-call | tf_op jit(solution)/shard_map/gather_halves/pallas_call | solution.py:462
  76.6 4.7 fusion.16
  86.2 9.8 %add_convert_fusion = bf16[2048,2304]{1,0:T(8,128)(2,1)} fusion(bf16[2048,768]{1,0:T(8,128)(2,1)S(1)} %bitcast.173, bf16[768,2304]{1,0:T(8,128)(2,1)S(1)} %bitcast.203, f32[2304]{0:T(1024)S(1)} %add.175), kind=kOutput, calls=%fused_computation.4 | convolution fusion | flops 7257194496 | bytes 16131072 | tf_op jit(solution)/shard_map/dot_general | solution.py:24
  96.0 56.5 %attention_forward.1 = (bf16[2,1024,768]{2,1,0:T(8,128)(2,1)S(1)}, f32[2,1024,768]{2,1,0:T(8,128)}) custom-call(s32[2,4,4]{2,1,0:T(4,128)S(1)} %pad_add_fusion.bounds, bf16[2,1024,2304]{2,1,0:T(8,128)(2,1)} %bitcast.206, bf16[2,1024,2304]{2,1,0:T(8,128)(2,1)} %bitcast.207, bf16[2,1024,2304]{2,1,0:T(8,128)(2,1)} %bitcast.208, ...), custom_call_target="tpu_custom_call" | custom-call | flops 25769803776 | bytes 18874368 | tf_op jit(solution)/shard_map/attention_forward/pallas_call | solution.py:258
  154.2 6.3 fusion.34
  164.0 19.2 %fusion.29 = f32[2048,3072]{1,0:T(8,128)} fusion(bf16[768,3072]{1,0:T(8,128)(2,1)} %all-gather.6.cloned.1.call-done, f32[2048,768]{1,0:T(8,128)} %copy-done.9, f32[768]{0:T(1024)S(1)} %add.183, f32[768]{0:T(1024)S(1)} %mul.195, f32[2048]{0:T(1024)S(1)} %add_rsqrt_fusion, f32[2048]{0:T(1024)S(1)} %broadcast_multiply_fusion.4), kind=kOutput, calls=%fused_computation.109 | convolution fusion | flops 9671540736 | bytes 36198400 | tf_op jit(solution)/shard_map/dot_general | solution.py:24
  183.2 21.3 %convolution_convert_fusion.1 = bf16[3072,768]{1,0:T(8,128)(2,1)} fusion(bf16[2048,768]{1,0:T(8,128)(2,1)S(1)} %copy-done.14, f32[2048,3072]{1,0:T(8,128)} %fusion.29, f32[3072]{0:T(1024)S(1)} %add.186), kind=kOutput, calls=%fused_computation.40 | convolution fusion | flops 9728950272 | bytes 33042432 | tf_op jit(solution)/shard_map/dot_general | solution.py:679
  204.5 17.0 %all-gather.8.cloned.1.call-done = bf16[3072,768]{1,0:T(8,128)(2,1)} async-done(((bf16[1536,768]{1,0:T(8,128)(2,1)}), bf16[3072,768]{1,0:T(8,128)(2,1)}) %all-gather.8.cloned.1.call-update) | async-done | bytes 4718608 | tf_op jit(solution)/shard_map/all_gather | solution.py:653
  221.5 26.8 %fusion.35 = (bf16[3072]{0:T(1024)(128)(2,1)S(1)}, bf16[2048,3072]{1,0:T(8,128)(2,1)}) fusion(f32[2048,3072]{1,0:T(8,128)} %fusion.29, f32[3072]{0:T(1024)S(1)} %add.186, bf16[2048,768]{1,0:T(8,128)(2,1)S(1)} %copy-done.14, bf16[3072,768]{1,0:T(8,128)(2,1)} %all-gather.8.cloned.1.call-done), kind=kOutput, calls=%fused_computation.115 | convolution fusion | flops 9789502464 | bytes 45631488 | tf_op jit(solution)/shard_map/dot_general | solution.py:28
  248.3 19.9 %convolution_convert_fusion = bf16[768,3072]{1,0:T(8,128)(2,1)} fusion(bf16[2048,3072]{1,0:T(8,128)(2,1)} %get-tuple-element.106, f32[2048,768]{1,0:T(8,128)} %copy-done.9, f32[768]{0:T(1024)S(1)} %add.183, f32[768]{0:T(1024)S(1)} %mul.195, f32[2048]{0:T(1024)S(1)} %add_rsqrt_fusion, f32[2048]{0:T(1024)S(1)} %broadcast_multiply_fusion.4), kind=kOutput, calls=%fused_computation.39 | convolution fusion | flops 9673900032 | bytes 23615488 | tf_op jit(solution)/shard_map/dot_general | solution.py:680
  268.2 18.1 %multiply_reduce_fusion.1 = (bf16[768]{0:T(1024)(128)(2,1)S(1)}, f32[2048]{0:T(1024)S(1)}, f32[2048]{0:T(1024)S(1)}, bf16[768]{0:T(1024)(128)(2,1)S(1)}, f32[2048,768]{1,0:T(8,128)}) fusion(f32[2048,768]{1,0:T(8,128)} %copy-done.9, f32[2048]{0:T(1024)S(1)} %add_rsqrt_fusion, f32[2048]{0:T(1024)S(1)} %broadcast_multiply_fusion.4, f32[768]{0:T(1024)S(1)} %mul.195, ...), kind=kOutput, calls=%fused_computation.27 | convolution fusion | flops 9677826048 | bytes 29923328 | tf_op jit(solution)/shard_map/dot_general | solution.py:28
  286.4 5.3 convert_reduce_fusion.1
  299.6 117.0 %attention_backward.1 = (bf16[3,2,1024,768]{3,2,1,0:T(8,128)(2,1)}, f32[2,8,768]{2,1,0:T(8,128)}) custom-call(s32[2,4,4]{2,1,0:T(4,128)} %copy-done.1, bf16[2,1024,2304]{2,1,0:T(8,128)(2,1)} %bitcast.209, bf16[2,1024,2304]{2,1,0:T(8,128)(2,1)} %bitcast.210, bf16[2,1024,2304]{2,1,0:T(8,128)(2,1)} %bitcast.211, bf16[2,1024,768]{2,1,0:T(8,128)(2,1)} %copy-done.3, ...), custom_call_target="tpu_custom_call" | custom-call | flops 64424509440 | bytes 31457280 | tf_op jit(solution)/shard_map/attention_backward/pallas_call | solution.py:298
  417.4 5.6 fusion.30
  426.8 4.7 fusion.20
  435.2 4.6 fusion.18
  439.8 9.8 %reshape.585 = bf16[2,384,4,768]{3,2,1,0:T(4,128)(2,1)} reshape(bf16[768,3072]{1,0:T(8,128)(2,1)} %convolution_convert_fusion) | data formatting | bytes 9437184 | tf_op jit(solution)/shard_map/reshape | solution.py:736
  449.6 5.1 copy.72
  455.1 6.7 convolution_convert_fusion.3
  461.8 9.8 %fusion.15 = (bf16[768]{0:T(1024)(128)(2,1)S(1)}, f32[2048]{0:T(1024)}, f32[2048]{0:T(1024)}, bf16[768]{0:T(1024)(128)(2,1)S(1)}, f32[2048,768]{1,0:T(8,128)}) fusion(bf16[2,1024,768]{2,1,0:T(8,128)(2,1)S(1)} %copy-done.6, f32[2048]{0:T(1024)S(1)} %copy-done.23, f32[2048]{0:T(1024)S(1)} %copy-done.25, f32[768]{0:T(1024)S(1)} %copy-done.21, ...), kind=kOutput, calls=%fused_computation.25 | convolution fusion | flops 2434787840 | bytes 26384384 | tf_op jit(solution)/shard_map/dot_general | solution.py:28
  477.7 198.5 %reduce_everywhere.1 = (bf16[4,2,2,96,768]{4,3,2,1,0:T(8,128)(2,1)}, bf16[4,2,2,96,768]{4,3,2,1,0:T(8,128)(2,1)}, bf16[4,2,2,112,768]{4,3,2,1,0:T(8,128)(2,1)}) custom-call(bf16[2,4,2,2,96,768]{5,4,3,2,1,0:T(8,128)(2,1)} %bitcast.165, bf16[2,4,2,2,96,768]{5,4,3,2,1,0:T(8,128)(2,1)} %bitcast.158, bf16[2,4,2,2,112,768]{5,4,3,2,1,0:T(8,128)(2,1)} %pad_maximum_fusion.refs_2_), custom_call_target="tpu_custom_call" | custom-call | tf_op jit(solution)/shard_map/reduce_everywhere/pallas_call | solution.py:582
  704.1 5.2 copy.79
  718.4 4.1 fusion.14
  722.5 23.5 %add_convert_fusion.1 = bf16[2048,768]{1,0:T(8,128)(2,1)} fusion(f32[2048,768]{1,0:T(8,128)} %copy-done.9, bf16[3072,768]{1,0:T(8,128)(2,1)} %all-gather.8.cloned.1.call-done, f32[768]{0:T(1024)S(1)} %copy-done.30, f32[2048,3072]{1,0:T(8,128)} %fusion.29, f32[3072]{0:T(1024)S(1)} %copy-done.28), kind=kOutput, calls=%fused_computation.31 | convolution fusion | flops 9731309568 | bytes 39336960 | tf_op jit(solution)/shard_map/dot_general | solution.py:24
  (195 shorter events, 81.2 us)
Async XLA Ops:
  7.2 64.1 %copy-start.31 = (s32[2,10]{1,0:T(2,128)S(1)}, s32[2,10]{1,0:T(2,128)}, u32[]{:S(2)}) copy-start(s32[2,10]{1,0:T(2,128)} %param.24) | copy-start | bytes 244
  7.2 66.1 %copy-start.5 = (bf16[2,1024,768]{2,1,0:T(8,128)(2,1)S(1)}, bf16[2,1024,768]{2,1,0:T(8,128)(2,1)}, u32[]{:S(2)}) copy-start(bf16[2,1024,768]{2,1,0:T(8,128)(2,1)} %param.13) | copy-start | bytes 9437188
  7.2 147.0 %all-gather.4.cloned.1.call-start = ((), (), s32[]{:S(2)}) async-start(), calls=%async_computation | async-start | bytes 1769472 | tf_op jit(solution)/shard_map/all_gather | solution.py:651
  69.8 94.2 %all-gather.6.cloned.1.call-start = ((), (), s32[]{:S(2)}) async-start(), calls=%async_computation.1 | async-start | bytes 7077888 | tf_op jit(solution)/shard_map/all_gather | solution.py:652
  70.5 151.0 %all-gather.8.cloned.1.call-start = ((), (), s32[]{:S(2)}) async-start(), calls=%async_computation.2 | async-start | bytes 7077888 | tf_op jit(solution)/shard_map/all_gather | solution.py:653
  76.6 19.4 %copy-start = (s32[2,1024,1]{2,1,0:T(8,128)}, s32[2,1024,1]{2,1,0:T(8,128)S(1)}, u32[]{:S(2)}) copy-start(s32[2,1024,1]{2,1,0:T(8,128)S(1)} %copy.70.pic_ref) | copy-start | bytes 24580
  81.5 14.5 %copy-start.2 = (f32[2,128]{1,0:T(2,128)}, f32[2,128]{1,0:T(2,128)S(1)}, u32[]{:S(2)}) copy-start(f32[2,128]{1,0:T(2,128)S(1)} %pad_maximum_fusion.5.gain_ref) | copy-start | bytes 3076
  81.6 139.9 %copy-start.27 = (f32[3072]{0:T(1024)}, f32[3072]{0:T(1024)S(1)}, u32[]{:S(2)}) copy-start(f32[3072]{0:T(1024)S(1)} %add.186) | copy-start | bytes 36868
  82.4 13.6 %copy-start.20 = (f32[768]{0:T(1024)}, f32[768]{0:T(1024)S(1)}, u32[]{:S(2)}) copy-start(f32[768]{0:T(1024)S(1)} %mul.189) | copy-start | bytes 9220
  83.1 12.9 %copy-start.1 = (s32[2,4,4]{2,1,0:T(4,128)}, s32[2,4,4]{2,1,0:T(4,128)S(1)}, u32[]{:S(2)}) copy-start(s32[2,4,4]{2,1,0:T(4,128)S(1)} %pad_add_fusion.bounds) | copy-start | bytes 388
  86.2 9.8 %copy-start.12 = (bf16[2,1024,768]{2,1,0:T(8,128)(2,1)}, bf16[2,1024,768]{2,1,0:T(8,128)(2,1)S(1)}, u32[]{:S(2)}) copy-start(bf16[2,1024,768]{2,1,0:T(8,128)(2,1)S(1)} %fusion.5) | copy-start | bytes 9437188
  163.9 19.3 %copy-start.14 = (bf16[2048,768]{1,0:T(8,128)(2,1)S(1)}, bf16[2048,768]{1,0:T(8,128)(2,1)}, u32[]{:S(2)}) copy-start(bf16[2048,768]{1,0:T(8,128)(2,1)} %fusion.16) | copy-start | bytes 9437188
  248.3 38.0 %slice-start = ((s8[6291456]{0:T(1024)(128)(4,1)}), s8[4194304]{0:T(1024)(128)(4,1)S(1)}, s32[]{:S(2)}) async-start(s8[6291456]{0:T(1024)(128)(4,1)} %bitcast.154), calls=%async_computation.3 | async-start | bytes 8388608
  268.2 18.2 %copy-start.8 = (bf16[2,1024,768]{2,1,0:T(8,128)(2,1)S(1)}, bf16[2,1024,768]{2,1,0:T(8,128)(2,1)}, u32[]{:S(2)}) copy-start(bf16[2,1024,768]{2,1,0:T(8,128)(2,1)} %param.25) | copy-start | bytes 9437188
  268.2 18.2 %slice-start.1 = ((s8[6291456]{0:T(1024)(128)(4,1)}), s8[2097152]{0:T(1024)(128)(4,1)S(1)}, s32[]{:S(2)}) async-start(s8[6291456]{0:T(1024)(128)(4,1)} %bitcast.154), calls=%async_computation.4 | async-start | bytes 4194304
  268.2 18.2 %copy-start.18 = (f32[1,8,2,128]{3,1,2,0:T(8,128)S(1)}, f32[1,8,2,128]{3,1,2,0:T(8,128)}, u32[]{:S(2)}) copy-start(f32[1,8,2,128]{3,1,2,0:T(8,128)} %copy-done.17) | copy-start | bytes 24580
  454.7 7.1 copy-start.6
  454.7 7.1 copy-start.21
  454.7 7.1 copy-start.23
  454.7 7.1 copy-start.25
  461.8 9.8 %copy-start.29 = (bf16[1,2,384]{2,1,0:T(2,128)(2,1)S(1)}, bf16[1,2,384]{2,1,0:T(2,128)(2,1)}, u32[]{:S(2)}) copy-start(bf16[1,2,384]{2,1,0:T(2,128)(2,1)} %stack.58) | copy-start | bytes 4612
  709.3 9.0 %slice-start.2 = ((s8[6291456]{0:T(1024)(128)(4,1)}), s8[4194304]{0:T(1024)(128)(4,1)S(1)}, s32[]{:S(2)}) async-start(s8[6291456]{0:T(1024)(128)(4,1)} %bitcast.156), calls=%async_computation.5 | async-start | bytes 8388608
  709.3 9.0 %slice-start.4 = ((s8[6291456]{0:T(1024)(128)(4,1)}), s8[4194304]{0:T(1024)(128)(4,1)S(1)}, s32[]{:S(2)}) async-start(s8[6291456]{0:T(1024)(128)(4,1)} %bitcast.162), calls=%async_computation.7 | async-start | bytes 8388608
  711.5 6.8 slice-start.3
  (21 other events, 98.8 us)
Sparse Core Ops, SparseCore 0:
  69.9 23.1 all-gather.3
  94.6 62.6 all-gather.5
  158.9 62.5 all-gather.7

commit v2 on v1

--- a/solution.py
+++ b/solution.py
@@ -458,7 +458,7 @@
 
 def gather_halves(fsdp, replicas, shards, pieces):
     copies = sum(len(item) for item in pieces) * (fsdp - 1)
-    any_space = pl.BlockSpec(memory_space=pl.ANY)
+    any_space = pl.BlockSpec(memory_space=pltpu.VMEM)
     return pl.pallas_call(
         functools.partial(gather_kernel, fsdp, replicas, pieces),
         name="gather_halves",
@@ -482,13 +482,11 @@
     lax.fori_loop(0, dst.shape[0], step, 0)
 
 
-def reduce_kernel(fsdp, replicas, count, *refs):
+def reduce_kernel(fsdp, replicas, count, chunks, *refs):
     grads, outs = refs[:count], refs[count : 2 * count]
-    from_core = refs[2 * count : 3 * count]
-    from_group = refs[3 * count : 4 * count]
-    from_side = refs[4 * count : 5 * count]
-    from_rest = refs[5 * count : 6 * count]
-    send, recv = refs[6 * count :]
+    parts = sum(len(chunk) for chunk in chunks)
+    buffers = refs[2 * count : -2]
+    send, recv = refs[-2:]
     me = Place(fsdp, replicas)
     rests = replicas // 4
     sibling = me.device(core=1 - me.core)
@@ -510,9 +508,18 @@
         return copy
 
     sent = []
-    flying = [None] * count
-
-    def stage(i, number):
+    flying = [None] * parts
+
+    def stage(i, part, number):
+        array, row, rows, col, cols = part
+        window = (pl.ds(row, rows), pl.ds(col, cols))
+        grad, out = grads[array], outs[array]
+        from_core, from_group, from_side, from_rest = (
+            buffers[i],
+            buffers[parts + i],
+            buffers[2 * parts + i],
+            buffers[3 * parts + i],
+        )
         if number > 0:
             for copy in flying[i]:
                 copy.wait_recv()
@@ -520,71 +527,74 @@
         begun = []
         if number == 0:
             for f in range(fsdp):
-                begun.append(
-                    start(grads[i].at[f, :, :, 1 - me.core], from_core[i].at[f], sibling)
-                )
+                for side in range(2):
+                    src = grad.at[(f, slice(None), side, 1 - me.core) + window]
+                    begun.append(start(src, from_core.at[f, :, side], sibling))
         elif number == 1:
             for f in range(fsdp):
                 for side in range(2):
-                    add_into(
-                        from_core[i].at[f, :, side],
-                        [grads[i].at[f, :, side, me.core], from_core[i].at[f, :, side]],
-                    )
+                    src = grad.at[(f, slice(None), side, me.core) + window]
+                    landed = from_core.at[f, :, side]
+                    add_into(landed, [src, landed])
             for k, f in enumerate(groups):
-                begun.append(start(from_core[i].at[f], from_group[i].at[k], me.device(f=f)))
+                begun.append(start(from_core.at[f], from_group.at[k], me.device(f=f)))
         elif number == 2:
             for side in range(2):
                 add_into(
-                    from_group[i].at[0, :, side],
-                    [from_core[i].at[me.f, :, side]]
-                    + [from_group[i].at[k, :, side] for k in range(fsdp - 1)],
+                    from_group.at[0, :, side],
+                    [from_core.at[me.f, :, side]]
+                    + [from_group.at[k, :, side] for k in range(fsdp - 1)],
                 )
-            begun.append(start(from_group[i].at[0, :, 1 - me.side], from_side[i], across))
+            begun.append(start(from_group.at[0, :, 1 - me.side], from_side, across))
         elif number == 3:
-            add_into(from_side[i], [from_group[i].at[0, :, me.side], from_side[i]])
+            add_into(from_side, [from_group.at[0, :, me.side], from_side])
             for k, rest in enumerate(others):
-                begun.append(
-                    start(from_side[i].at[rest], from_rest[i].at[k], me.device(rest=rest))
-                )
+                begun.append(start(from_side.at[rest], from_rest.at[k], me.device(rest=rest)))
         elif number == 4:
-            mine = outs[i].at[pl.ds(me.rest, 1), me.side, me.core]
+            mine = out.at[(pl.ds(me.rest, 1), me.side, me.core) + window]
             add_into(
                 mine,
-                [from_side[i].at[pl.ds(me.rest, 1)]]
-                + [from_rest[i].at[pl.ds(k, 1)] for k in range(rests - 1)],
+                [from_side.at[pl.ds(me.rest, 1)]]
+                + [from_rest.at[pl.ds(k, 1)] for k in range(rests - 1)],
             )
             for rest in others:
                 begun.append(start(mine, mine, me.device(rest=rest)))
         elif number == 5:
-            mine = outs[i].at[:, me.side, me.core]
+            mine = out.at[(slice(None), me.side, me.core) + window]
             begun.append(start(mine, mine, across))
         elif number == 6:
-            mine = outs[i].at[:, :, me.core]
-            begun.append(start(mine, mine, sibling))
+            for side in range(2):
+                mine = out.at[(slice(None), side, me.core) + window]
+                begun.append(start(mine, mine, sibling))
         flying[i] = begun
 
     stages = 8
-    for tick in range(stages + count - 1):
-        for i in range(count):
-            number = tick - i
-            if 0 <= number < stages:
-                stage(i, number)
+    for tick in range(stages + len(chunks) - 1):
+        i = 0
+        for c, chunk in enumerate(chunks):
+            number = tick - c
+            for part in chunk:
+                if 0 <= number < stages:
+                    stage(i, part, number)
+                i += 1
     for copy in sent:
         copy.wait_send()
 
 
-def reduce_everywhere(fsdp, replicas, grads):
+def reduce_everywhere(fsdp, replicas, grads, chunks):
     rests = replicas // 4
     count = len(grads)
-    tails = [item.shape[-2:] for item in grads]
-    copies = count * (fsdp + (fsdp - 1) + 1 + (rests - 1) + (rests - 1) + 2)
+    tails = [(part[2], part[4]) for chunk in chunks for part in chunk]
+    copies = len(tails) * (2 * fsdp + (fsdp - 1) + 1 + (rests - 1) + (rests - 1) + 3)
     vmem = pl.BlockSpec(memory_space=pltpu.VMEM)
     return pl.pallas_call(
-        functools.partial(reduce_kernel, fsdp, replicas, count),
+        functools.partial(reduce_kernel, fsdp, replicas, count, chunks),
         name="reduce_everywhere",
         in_specs=[vmem] * count,
         out_specs=[vmem] * count,
-        out_shape=[jax.ShapeDtypeStruct((rests, 2, 2) + tail, bf16) for tail in tails],
+        out_shape=[
+            jax.ShapeDtypeStruct((rests, 2, 2) + item.shape[-2:], bf16) for item in grads
+        ],
         scratch_shapes=[pltpu.VMEM((fsdp, rests, 2) + tail, bf16) for tail in tails]
         + [pltpu.VMEM((fsdp - 1, rests, 2) + tail, bf16) for tail in tails]
         + [pltpu.VMEM((rests,) + tail, bf16) for tail in tails]
@@ -721,32 +731,26 @@
         axis=1,
     ).astype(bf16)
     lead = (fsdp, replicas // 4, 2, 2)
-    hidden_blocks = w_in.shape[1] // width
     small_rows = 16
     flat_grads = jnp.pad(
-        flat_grads, ((0, 0), (0, replicas * small_rows * width - flat_grads.shape[1]))
-    )
-    qkv_rows = jnp.stack(grad_w_qkv).reshape(3, fsdp, shard_rows, width)
-    qkv_rows = jnp.swapaxes(qkv_rows, 0, 1).reshape(lead + (-1, width))
-    proj_rows = grad_w_proj.reshape(lead + (-1, width))
-    last_rows = [proj_rows, qkv_rows, flat_grads.reshape(lead + (small_rows, width))]
-    last_sizes = [item.shape[-2] for item in last_rows]
-    spare = -sum(last_sizes) % 16
-    last_rows.append(jnp.zeros(lead + (spare, width), bf16))
-    in_rows = grad_w_in.reshape(fsdp, shard_rows, hidden_blocks, width)
-    in_rows = jnp.moveaxis(in_rows, 2, 1).reshape(lead + (-1, width))
-    out_rows = grad_w_out.reshape(lead + (-1, width))
-    r_out, r_in, r_last = reduce_everywhere(
-        fsdp, replicas, [out_rows, in_rows, jnp.concatenate(last_rows, axis=-2)]
-    )
-    r_w_out = r_out.reshape(-1, width)
-    r_w_in = jnp.moveaxis(r_in.reshape(hidden_blocks, shard_rows, width), 0, 1)
-    r_w_in = r_w_in.reshape(shard_rows, -1)
-    first, second = last_sizes[0], last_sizes[0] + last_sizes[1]
-    r_w_proj = r_last[..., :first, :].reshape(-1, width)
-    r_w_qkv = r_last[..., first:second, :].reshape(3, shard_rows, width)
-    r_w_qkv = jnp.swapaxes(r_w_qkv, 0, 1).reshape(shard_rows, columns)
-    r_flat = r_last[..., second : second + small_rows, :].reshape(-1).astype(f32)
+        flat_grads, ((0, 0), (0, replicas * small_rows * PAIR - flat_grads.shape[1]))
+    )
+    payload = [grad_w_out, grad_w_in, *grad_w_qkv, grad_w_proj]
+    payload = [item.reshape(lead + (-1, item.shape[-1])) for item in payload]
+    payload.append(flat_grads.reshape(lead + (small_rows, PAIR)))
+    whole = [(i, 0, item.shape[-2], 0, item.shape[-1]) for i, item in enumerate(payload)]
+    out_half, in_half = whole[0][2] // 2, whole[1][4] // 2
+    out_chunks = [[whole[0]]]
+    if out_half % 16 == 0:
+        out_chunks = [[(0, at, out_half, 0, width)] for at in (0, out_half)]
+    in_chunks = [[(1, 0, whole[1][2], at, in_half)] for at in (0, in_half)]
+    chunks = out_chunks + in_chunks + [[whole[2], whole[3]], [whole[4], whole[5], whole[6]]]
+    reduced = reduce_everywhere(fsdp, replicas, payload, chunks)
+    r_w_out, r_w_in, r_q, r_k, r_v, r_w_proj = (
+        item.reshape(-1, item.shape[-1]) for item in reduced[:6]
+    )
+    r_w_qkv = jnp.concatenate([r_q, r_k, r_v], axis=1)
+    r_flat = reduced[6].reshape(-1).astype(f32)
     r_small = []
     at = 0
     for item in small:

time: 759 us -> 651 us (0.86)
  Pallas kernels: 429 us -> 372 us
  local copies, waits for them, and re-layouts: 64.6 us -> 26.5 us
    pallas_call x1, Pallas kernels: 198 us -> 167 us  [reduce_everywhere(): pl.pallas_call(functools.partial(reduce_kernel, fsdp, replicas, count, ch...]
    pallas_call x1, Pallas kernels: 57.4 us -> 28 us  [gather_halves(): pl.pallas_call(functools.partial(gather_kernel, fsdp, replicas, pieces),...]
    reshape x2 -> x0, local copies, waits for them, and re-layouts: 14.9 us -> none  [on_device(): in_rows = grad_w_in.reshape(fsdp, shard_rows, hidden_blocks, width)]
    convert_element_type x5 -> x1, local copies, waits for them, and re-layouts: 13.5 us -> 0.99 us  [on_device(): r_flat = reduced[6].reshape(-1).astype(f32)]
  transfers between devices with their start and end apart: 3 -> 3, of which waited for: 1 -> 1; matrix products, arithmetic and copies ran while one was open for 10% -> 11% of each run, Pallas kernels for 8% -> 10%
where the time goes in v2:
time: 651 us; the launch traced here: 646 us
  Pallas kernels  372 us (57%)
  matrix products  185 us (28%)
  other arithmetic  36 us (6%)
  local copies, waits for them, and re-layouts  26.5 us (4%)
  between operations  14.7 us (2%)
  waiting for transfers between devices  12 us (2%)
    pallas_call x1, Pallas kernels, reduce_everywhere(): pl.pallas_call(functools.partial(reduce_kernel, fsdp, replicas, count, ch...  167 us
    pallas_call x1, Pallas kernels, attention_back(): pl.pallas_call(backward_kernel, name='attention_backward', grid_spec=pltp...  114 us
    dot_general x6, matrix products, dot_nt(): return lax.dot_general(a, b, NT, preferred_element_type=f32)  67.6 us
    pallas_call x1, Pallas kernels, attention(): pl.pallas_call(forward_kernel, name='attention_forward', grid_spec=pltpu....  63 us
    dot_general x4, matrix products, dot(): return jnp.dot(a, b, preferred_element_type=f32)  58.2 us
    pallas_call x1, Pallas kernels, gather_halves(): pl.pallas_call(functools.partial(gather_kernel, fsdp, replicas, pieces),...  28 us
    dot_general x1, matrix products, on_device(): lax.dot_general(activated, grad_mlp, tt, preferred_element_type=f32)  21.3 us
    dot_general x1, matrix products, on_device(): lax.dot_general(normed2, grad_hidden, tt, preferred_element_type=f32)  19.9 us
  transfers between devices with their start and end apart: 3, of which 1 were waited for; matrix products, arithmetic and copies ran while one was open for 11% of the time, Pallas kernels for 10%

profile of v2, /device:TPU:1, one launch (start us, length us, event | category | flops | bytes accessed | tf_op | source)
XLA Modules:
  0.0 645.9 jit_solution(9398572861160757211)
XLA Ops:
  12.3 28.0 %gather_halves.1 = (bf16[2,2,192,2304]{3,2,1,0:T(8,128)(2,1)}, bf16[2,2,16,256]{3,2,1,0:T(8,128)(2,1)}) custom-call(bf16[2,192,2304]{2,1,0:T(8,128)(2,1)} %bitcast.153, bf16[2,16,256]{2,1,0:T(8,128)(2,1)} %reshape.566.refs_1_), custom_call_target="tpu_custom_call" | custom-call | tf_op jit(solution)/shard_map/gather_halves/pallas_call | solution.py:462
  47.2 4.7 fusion.16
  56.8 9.8 %add_convert_fusion = bf16[2048,2304]{1,0:T(8,128)(2,1)} fusion(bf16[2048,768]{1,0:T(8,128)(2,1)S(1)} %bitcast.149, bf16[768,2304]{1,0:T(8,128)(2,1)S(1)} %bitcast.184, f32[2304]{0:T(1024)S(1)} %add.175), kind=kOutput, calls=%fused_computation.4 | convolution fusion | flops 7257194496 | bytes 16131072 | tf_op jit(solution)/shard_map/dot_general | solution.py:24
  66.6 63.0 %attention_forward.1 = (bf16[2,1024,768]{2,1,0:T(8,128)(2,1)S(1)}, f32[2,1024,768]{2,1,0:T(8,128)}) custom-call(s32[2,4,4]{2,1,0:T(4,128)S(1)} %pad_add_fusion.bounds, bf16[2,1024,2304]{2,1,0:T(8,128)(2,1)} %bitcast.187, bf16[2,1024,2304]{2,1,0:T(8,128)(2,1)} %bitcast.188, bf16[2,1024,2304]{2,1,0:T(8,128)(2,1)} %bitcast.189, ...), custom_call_target="tpu_custom_call" | custom-call | flops 25769803776 | bytes 18874368 | tf_op jit(solution)/shard_map/attention_forward/pallas_call | solution.py:258
  131.2 6.3 fusion.33
  141.3 18.7 %fusion.29 = f32[2048,3072]{1,0:T(8,128)} fusion(bf16[768,3072]{1,0:T(8,128)(2,1)} %all-gather.6.cloned.1.call-done, f32[2048,768]{1,0:T(8,128)} %copy-done.9, f32[768]{0:T(1024)S(1)} %add.183, f32[768]{0:T(1024)S(1)} %mul.195, f32[2048]{0:T(1024)S(1)} %add_rsqrt_fusion, f32[2048]{0:T(1024)S(1)} %broadcast_multiply_fusion.4), kind=kOutput, calls=%fused_computation.108 | convolution fusion | flops 9671540736 | bytes 36198400 | tf_op jit(solution)/shard_map/dot_general | solution.py:24
  160.0 21.3 %convolution_convert_fusion.1 = bf16[3072,768]{1,0:T(8,128)(2,1)} fusion(bf16[2048,768]{1,0:T(8,128)(2,1)S(1)} %copy-done.14, f32[2048,3072]{1,0:T(8,128)} %fusion.29, f32[3072]{0:T(1024)S(1)} %add.186), kind=kOutput, calls=%fused_computation.39 | convolution fusion | flops 9728950272 | bytes 33042432 | tf_op jit(solution)/shard_map/dot_general | solution.py:689
  181.2 10.6 %all-gather.8.cloned.1.call-done = bf16[3072,768]{1,0:T(8,128)(2,1)} async-done(((bf16[1536,768]{1,0:T(8,128)(2,1)}), bf16[3072,768]{1,0:T(8,128)(2,1)}) %all-gather.8.cloned.1.call-update) | async-done | bytes 4718608 | tf_op jit(solution)/shard_map/all_gather | solution.py:663
  191.8 26.8 %fusion.34 = (bf16[3072]{0:T(1024)(128)(2,1)S(1)}, bf16[2048,3072]{1,0:T(8,128)(2,1)}) fusion(f32[2048,3072]{1,0:T(8,128)} %fusion.29, f32[3072]{0:T(1024)S(1)} %add.186, bf16[2048,768]{1,0:T(8,128)(2,1)S(1)} %copy-done.14, bf16[3072,768]{1,0:T(8,128)(2,1)} %all-gather.8.cloned.1.call-done), kind=kOutput, calls=%fused_computation.113 | convolution fusion | flops 9789502464 | bytes 45631488 | tf_op jit(solution)/shard_map/dot_general | solution.py:28
  218.6 19.9 %convolution_convert_fusion = bf16[768,3072]{1,0:T(8,128)(2,1)} fusion(bf16[2048,3072]{1,0:T(8,128)(2,1)} %get-tuple-element.89, f32[2048,768]{1,0:T(8,128)} %copy-done.9, f32[768]{0:T(1024)S(1)} %add.183, f32[768]{0:T(1024)S(1)} %mul.195, f32[2048]{0:T(1024)S(1)} %add_rsqrt_fusion, f32[2048]{0:T(1024)S(1)} %broadcast_multiply_fusion.4), kind=kOutput, calls=%fused_computation.38 | convolution fusion | flops 9673900032 | bytes 23615488 | tf_op jit(solution)/shard_map/dot_general | solution.py:690
  238.5 18.1 %multiply_reduce_fusion.1 = (bf16[768]{0:T(1024)(128)(2,1)S(1)}, f32[2048]{0:T(1024)S(1)}, f32[2048]{0:T(1024)S(1)}, bf16[768]{0:T(1024)(128)(2,1)S(1)}, f32[2048,768]{1,0:T(8,128)}) fusion(f32[2048,768]{1,0:T(8,128)} %copy-done.9, f32[2048]{0:T(1024)S(1)} %add_rsqrt_fusion, f32[2048]{0:T(1024)S(1)} %broadcast_multiply_fusion.4, f32[768]{0:T(1024)S(1)} %mul.195, ...), kind=kOutput, calls=%fused_computation.27 | convolution fusion | flops 9677826048 | bytes 29923328 | tf_op jit(solution)/shard_map/dot_general | solution.py:28
  256.7 5.3 convert_reduce_fusion.1
  262.1 3.8 convolution_convert_fusion.3
  266.0 4.0 convolution_convert_fusion.2
  270.0 113.8 %attention_backward.1 = (bf16[3,2,1024,768]{3,2,1,0:T(8,128)(2,1)}, f32[2,8,768]{2,1,0:T(8,128)}) custom-call(s32[2,4,4]{2,1,0:T(4,128)} %copy-done.1, bf16[2,1024,2304]{2,1,0:T(8,128)(2,1)} %bitcast.190, bf16[2,1024,2304]{2,1,0:T(8,128)(2,1)} %bitcast.191, bf16[2,1024,2304]{2,1,0:T(8,128)(2,1)} %bitcast.192, bf16[2,1024,768]{2,1,0:T(8,128)(2,1)} %copy-done.3, ...), custom_call_target="tpu_custom_call" | custom-call | flops 64424509440 | bytes 31457280 | tf_op jit(solution)/shard_map/attention_backward/pallas_call | solution.py:298
  384.6 5.6 fusion.30
  393.9 4.7 fusion.20
  402.4 4.6 fusion.18
  407.4 6.7 %convolution_convert_fusion.4 = bf16[768,768]{1,0:T(8,128)(2,1)} fusion(bf16[2048,768]{1,0:T(8,128)(2,1)} %bitcast.150, bf16[2048,768]{1,0:T(8,128)(2,1)} %bitcast.143), kind=kOutput, calls=%fused_computation.45 | convolution fusion | flops 2416508928 | bytes 7471104 | tf_op jit(solution)/shard_map/dot_general | solution.py:709
  414.2 9.2 %fusion.15 = (bf16[768]{0:T(1024)(128)(2,1)S(1)}, f32[2048]{0:T(1024)S(1)}, f32[2048]{0:T(1024)S(1)}, bf16[768]{0:T(1024)(128)(2,1)S(1)}, f32[2048,768]{1,0:T(8,128)}) fusion(bf16[2,1024,768]{2,1,0:T(8,128)(2,1)S(1)} %copy-done.6, f32[2048]{0:T(1024)S(1)} %copy-done.24, f32[2048]{0:T(1024)S(1)} %copy-done.25, f32[768]{0:T(1024)S(1)} %copy-done.23, ...), kind=kOutput, calls=%fused_computation.25 | convolution fusion | flops 2434787840 | bytes 26384384 | tf_op jit(solution)/shard_map/dot_general | solution.py:28
  424.4 166.8 %reduce_everywhere.1 = (bf16[4,2,2,96,768]{4,3,2,1,0:T(8,128)(2,1)}, bf16[4,2,2,24,3072]{4,3,2,1,0:T(8,128)(2,1)}, bf16[4,2,2,24,768]{4,3,2,1,0:T(8,128)(2,1)}, ...) custom-call(bf16[2,4,2,2,96,768]{5,4,3,2,1,0:T(8,128)(2,1)} %bitcast, ...), custom_call_target="tpu_custom_call" | custom-call | tf_op jit(solution)/shard_map/reduce_everywhere/pallas_call | solution.py:590
  600.3 4.6 bitcast_convert_fusion.1
  607.7 5.8 fusion.14
  615.5 23.4 %add_convert_fusion.1 = bf16[2048,768]{1,0:T(8,128)(2,1)} fusion(f32[2048,768]{1,0:T(8,128)} %copy-done.9, bf16[3072,768]{1,0:T(8,128)(2,1)} %all-gather.8.cloned.1.call-done, f32[768]{0:T(1024)S(1)} %copy-done.29, f32[2048,3072]{1,0:T(8,128)} %fusion.29, f32[3072]{0:T(1024)S(1)} %copy-done.27), kind=kOutput, calls=%fused_computation.31 | convolution fusion | flops 9731309568 | bytes 39336960 | tf_op jit(solution)/shard_map/dot_general | solution.py:24
  (178 shorter events, 45.6 us)
Async XLA Ops:
  7.2 34.7 %copy-start.30 = (s32[2,10]{1,0:T(2,128)S(1)}, s32[2,10]{1,0:T(2,128)}, u32[]{:S(2)}) copy-start(s32[2,10]{1,0:T(2,128)} %param.24) | copy-start | bytes 244
  7.2 36.6 %copy-start.5 = (bf16[2,1024,768]{2,1,0:T(8,128)(2,1)S(1)}, bf16[2,1024,768]{2,1,0:T(8,128)(2,1)}, u32[]{:S(2)}) copy-start(bf16[2,1024,768]{2,1,0:T(8,128)(2,1)} %param.13) | copy-start | bytes 9437188
  7.2 124.0 %all-gather.4.cloned.1.call-start = ((), (), s32[]{:S(2)}) async-start(), calls=%async_computation | async-start | bytes 1769472 | tf_op jit(solution)/shard_map/all_gather | solution.py:661
  40.4 100.9 %all-gather.6.cloned.1.call-start = ((), (), s32[]{:S(2)}) async-start(), calls=%async_computation.1 | async-start | bytes 7077888 | tf_op jit(solution)/shard_map/all_gather | solution.py:662
  41.1 150.7 %all-gather.8.cloned.1.call-start = ((), (), s32[]{:S(2)}) async-start(), calls=%async_computation.2 | async-start | bytes 7077888 | tf_op jit(solution)/shard_map/all_gather | solution.py:663
  47.2 19.4 %copy-start = (s32[2,1024,1]{2,1,0:T(8,128)}, s32[2,1024,1]{2,1,0:T(8,128)S(1)}, u32[]{:S(2)}) copy-start(s32[2,1024,1]{2,1,0:T(8,128)S(1)} %copy.57.pic_ref) | copy-start | bytes 24580
  52.1 14.5 %copy-start.2 = (f32[2,128]{1,0:T(2,128)}, f32[2,128]{1,0:T(2,128)S(1)}, u32[]{:S(2)}) copy-start(f32[2,128]{1,0:T(2,128)S(1)} %pad_maximum_fusion.3.gain_ref) | copy-start | bytes 3076
  52.1 139.7 %copy-start.26 = (f32[3072]{0:T(1024)}, f32[3072]{0:T(1024)S(1)}, u32[]{:S(2)}) copy-start(f32[3072]{0:T(1024)S(1)} %add.186) | copy-start | bytes 36868
  52.9 13.6 %copy-start.22 = (f32[768]{0:T(1024)}, f32[768]{0:T(1024)S(1)}, u32[]{:S(2)}) copy-start(f32[768]{0:T(1024)S(1)} %mul.189) | copy-start | bytes 9220
  53.6 12.9 %copy-start.1 = (s32[2,4,4]{2,1,0:T(4,128)}, s32[2,4,4]{2,1,0:T(4,128)S(1)}, u32[]{:S(2)}) copy-start(s32[2,4,4]{2,1,0:T(4,128)S(1)} %pad_add_fusion.bounds) | copy-start | bytes 388
  56.7 9.8 %copy-start.12 = (bf16[2,1024,768]{2,1,0:T(8,128)(2,1)}, bf16[2,1024,768]{2,1,0:T(8,128)(2,1)S(1)}, u32[]{:S(2)}) copy-start(bf16[2,1024,768]{2,1,0:T(8,128)(2,1)S(1)} %fusion.5) | copy-start | bytes 9437188
  141.2 18.7 %copy-start.14 = (bf16[2048,768]{1,0:T(8,128)(2,1)S(1)}, bf16[2048,768]{1,0:T(8,128)(2,1)}, u32[]{:S(2)}) copy-start(bf16[2048,768]{1,0:T(8,128)(2,1)} %fusion.16) | copy-start | bytes 9437188
  218.6 38.0 %slice-start = ((s8[6291456]{0:T(1024)(128)(4,1)}), s8[4194304]{0:T(1024)(128)(4,1)S(1)}, s32[]{:S(2)}) async-start(s8[6291456]{0:T(1024)(128)(4,1)} %bitcast.136), calls=%async_computation.3 | async-start | bytes 8388608
  238.5 18.2 %copy-start.8 = (bf16[2,1024,768]{2,1,0:T(8,128)(2,1)S(1)}, bf16[2,1024,768]{2,1,0:T(8,128)(2,1)}, u32[]{:S(2)}) copy-start(bf16[2,1024,768]{2,1,0:T(8,128)(2,1)} %param.25) | copy-start | bytes 9437188
  238.5 18.2 %slice-start.1 = ((s8[6291456]{0:T(1024)(128)(4,1)}), s8[2097152]{0:T(1024)(128)(4,1)S(1)}, s32[]{:S(2)}) async-start(s8[6291456]{0:T(1024)(128)(4,1)} %bitcast.136), calls=%async_computation.4 | async-start | bytes 4194304
  238.5 18.2 %copy-start.20 = (f32[1,8,2,128]{3,1,2,0:T(8,128)S(1)}, f32[1,8,2,128]{3,1,2,0:T(8,128)}, u32[]{:S(2)}) copy-start(f32[1,8,2,128]{3,1,2,0:T(8,128)} %copy-done.19) | copy-start | bytes 24580
  407.0 7.1 %copy-start.24 = (f32[2048]{0:T(1024)S(1)}, f32[2048]{0:T(1024)}, u32[]{:S(2)}) copy-start(f32[2048]{0:T(1024)} %get-tuple-element.92) | copy-start | bytes 24580
  407.0 7.1 %copy-start.25 = (f32[2048]{0:T(1024)S(1)}, f32[2048]{0:T(1024)}, u32[]{:S(2)}) copy-start(f32[2048]{0:T(1024)} %get-tuple-element.93) | copy-start | bytes 24580
  414.2 9.3 %copy-start.28 = (bf16[1,2,384]{2,1,0:T(2,128)(2,1)S(1)}, bf16[1,2,384]{2,1,0:T(2,128)(2,1)}, u32[]{:S(2)}) copy-start(bf16[1,2,384]{2,1,0:T(2,128)(2,1)} %stack.42) | copy-start | bytes 4612
  597.5 7.4 %copy-start.15 = (bf16[4,2,2,96,768]{4,3,2,1,0:T(8,128)(2,1)S(1)}, bf16[4,2,2,96,768]{4,3,2,1,0:T(8,128)(2,1)}, u32[]{:S(2)}) copy-start(bf16[4,2,2,96,768]{4,3,2,1,0:T(8,128)(2,1)} %get-tuple-element.45) | copy-start | bytes 7077892
  598.0 9.6 %slice-start.2 = ((s8[6291456]{0:T(1024)(128)(4,1)}), s8[4194304]{0:T(1024)(128)(4,1)S(1)}, s32[]{:S(2)}) async-start(s8[6291456]{0:T(1024)(128)(4,1)} %bitcast.138), calls=%async_computation.5 | async-start | bytes 8388608
  600.3 7.3 %slice-start.3 = ((s8[6291456]{0:T(1024)(128)(4,1)}), s8[2097152]{0:T(1024)(128)(4,1)S(1)}, s32[]{:S(2)}) async-start(s8[6291456]{0:T(1024)(128)(4,1)} %bitcast.138), calls=%async_computation.6 | async-start | bytes 4194304
  607.6 7.9 %copy-start.27 = (f32[3072]{0:T(1024)S(1)}, f32[3072]{0:T(1024)}, u32[]{:S(2)}) copy-start(f32[3072]{0:T(1024)} %copy-done.26) | copy-start | bytes 36868
  607.7 7.9 %copy-start.29 = (f32[768]{0:T(1024)S(1)}, f32[768]{0:T(1024)}, u32[]{:S(2)}) copy-start(f32[768]{0:T(1024)} %add.192) | copy-start | bytes 9220
  (18 other events, 87.9 us)
Sparse Core Ops, SparseCore 0:
  40.5 22.8 all-gather.3
  64.9 62.6 all-gather.5
  129.1 62.6 all-gather.7

commit v3 on v2

--- a/solution.py
+++ b/solution.py
@@ -11,7 +11,7 @@
 H = 12
 HD = 64
 PAIR = 2 * HD
-GROUP = 3
+GROUP = 6
 BLK = 256
 MASK = 256.0
 LOG2E = math.log2(math.e)
@@ -39,12 +39,12 @@
     return jnp.where(hit, value, 0.0).astype(bf16)
 
 
-def head_stats(raw, averager):
-    mean = dot(raw, averager)
-    centered = raw.astype(f32) - mean
-    variance = dot((centered * centered).astype(bf16), averager)
-    rstd = lax.rsqrt(variance + 1e-6)
-    return centered * rstd, rstd
+def head_stats(raws, averager):
+    means = [dot(raw, averager) for raw in raws]
+    centered = [raw.astype(f32) - mean for raw, mean in zip(raws, means)]
+    variances = [dot((item * item).astype(bf16), averager) for item in centered]
+    rstds = [lax.rsqrt(item + 1e-6) for item in variances]
+    return [item * rstd for item, rstd in zip(centered, rstds)], rstds
 
 
 def split(v):
@@ -81,12 +81,12 @@
         pic = pic_ref[0, at, :]
         q_more = query_extra(pic, lane)
         k_more = key_extra(pic, lane)
-        for p in range(GROUP):
-            col = slice(p * PAIR, (p + 1) * PAIR)
-            normed, _unused = head_stats(q_ref[0, at, col], averager)
-            q = (normed * gain_ref[0:1, :]).astype(bf16).astype(f32) * 0.125
-            normed, _unused = head_stats(k_ref[0, at, col], averager)
-            k = normed * gain_ref[1:2, :]
+        cols = [slice(p * PAIR, (p + 1) * PAIR) for p in range(GROUP)]
+        raws = [q_ref[0, at, col] for col in cols] + [k_ref[0, at, col] for col in cols]
+        normed, _unused = head_stats(raws, averager)
+        for p, col in enumerate(cols):
+            q = (normed[p] * gain_ref[0:1, :]).astype(bf16).astype(f32) * 0.125
+            k = normed[GROUP + p] * gain_ref[1:2, :]
             v = v_ref[0, at, col].astype(f32)
             qa[2 * p, at, :] = jnp.where(low_half, q, q_more).astype(bf16)
             qa[2 * p + 1, at, :] = jnp.where(low_half, q_more, q).astype(bf16)
@@ -104,9 +104,11 @@
 
         def key_block(kb, _):
             keys = pl.ds(pl.multiple_of(kb * BLK, BLK), BLK)
+            ahead = [dot_nt(qa[0, at, :], ka[0, keys, :])]
             for h in range(heads):
-                scores = dot_nt(qa[h, at, :], ka[h, keys, :])
-                probs = jnp.exp2(scores * LOG2E).astype(bf16)
+                if h + 1 < heads:
+                    ahead.append(dot_nt(qa[h + 1, at, :], ka[h + 1, keys, :]))
+                probs = jnp.exp2(ahead[h] * LOG2E).astype(bf16)
                 acc[h] += dot(probs, va[h, keys, :])
             return 0
 
@@ -159,19 +161,20 @@
         pic = pic_ref[0, at, :]
         q_hot = query_extra(pic, lane)
         k_more = key_extra(pic, lane)
-        for p in range(GROUP):
-            col = slice(p * PAIR, (p + 1) * PAIR)
+        cols = [slice(p * PAIR, (p + 1) * PAIR) for p in range(GROUP)]
+        raws = [q_ref[0, at, col] for col in cols] + [k_ref[0, at, col] for col in cols]
+        normed, _unused = head_stats(raws, averager)
+        grads = [g_ref[0, at, col].astype(f32) for col in cols]
+        parts = [split(g * o_ref[0, at, col].astype(f32)) for g, col in zip(grads, cols)]
+        centres = [dot(high, crosser) + dot(low, crosser) for high, low in parts]
+        for p, col in enumerate(cols):
             lse = lse_ref[0, at, col]
             lse_high = lse.astype(bf16).astype(f32)
             q_more = jnp.where(slot == 12, lse_high, jnp.where(slot == 13, lse - lse_high, q_hot))
-            normed, _unused = head_stats(q_ref[0, at, col], averager)
-            q = (normed * gain_ref[0:1, :]).astype(bf16).astype(f32) * 0.125
-            normed, _unused = head_stats(k_ref[0, at, col], averager)
-            k = normed * gain_ref[1:2, :]
+            q = (normed[p] * gain_ref[0:1, :]).astype(bf16).astype(f32) * 0.125
+            k = normed[GROUP + p] * gain_ref[1:2, :]
             v = v_ref[0, at, col].astype(f32)
-            g = g_ref[0, at, col].astype(f32)
-            high, low = split(g * o_ref[0, at, col].astype(f32))
-            centre = dot(high, crosser) + dot(low, crosser)
+            g, centre = grads[p], centres[p]
             centre_high = centre.astype(bf16).astype(f32)
             g_more = jnp.where(
                 slot == 12, centre_high, jnp.where(slot == 13, centre - centre_high, 0.0)
@@ -192,13 +195,20 @@
     dqt[...] = jnp.zeros_like(dqt)
     stat_ref[...] = jnp.zeros_like(stat_ref)
 
-    def pull_norm(raw, grad, gain):
-        normed, rstd = head_stats(raw, averager)
-        lifted = grad * gain
-        mean_one = dot(lifted.astype(bf16), averager)
-        mean_two = dot((lifted * normed).astype(bf16), averager)
-        raw_grad = rstd * (lifted - mean_one - normed * mean_two)
-        return raw_grad.astype(bf16), jnp.sum(grad * normed, axis=0, keepdims=True)
+    cols = [slice(p * PAIR, (p + 1) * PAIR) for p in range(GROUP)]
+
+    def pull_norm(raws, grads, gain):
+        normed, rstds = head_stats(raws, averager)
+        lifted = [grad * gain for grad in grads]
+        ones = [dot(item.astype(bf16), averager) for item in lifted]
+        twos = [dot((a * n).astype(bf16), averager) for a, n in zip(lifted, normed)]
+        raw_grads = [
+            (rstd * (a - one - n * two)).astype(bf16)
+            for rstd, a, one, n, two in zip(rstds, lifted, ones, normed, twos)
+        ]
+        return raw_grads, [
+            jnp.sum(grad * n, axis=0, keepdims=True) for grad, n in zip(grads, normed)
+        ]
 
     def key_block(b, _):
         keys = pl.ds(pl.multiple_of(b * BLK, BLK), BLK)
@@ -207,11 +217,19 @@
 
         def query_block(qb, _):
             at = pl.ds(pl.multiple_of(qb * BLK, BLK), BLK)
+            def first(h):
+                return (
+                    dot_nt(ka[h, keys, :], qa[h, at, :]),
+                    dot_nt(va[h, keys, :], ga[h, at, :]),
+                )
+
+            ahead = [first(0)]
             for h in range(heads):
                 p, half = h // 2, slice((h % 2) * HD, (h % 2 + 1) * HD)
-                scores = dot_nt(ka[h, keys, :], qa[h, at, :])
+                if h + 1 < heads:
+                    ahead.append(first(h + 1))
+                scores, pulls = ahead[h]
                 probs = jnp.exp2(scores * LOG2E)
-                pulls = dot_nt(va[h, keys, :], ga[h, at, :])
                 grads = (probs * pulls).astype(bf16)
                 dv[h] += dot(probs.astype(bf16), ga[h, at, :])
                 dk[h] += dot(grads, qa[h, at, :])
@@ -219,12 +237,14 @@
             return 0
 
         lax.fori_loop(bounds[row, 2, b], bounds[row, 3, b], query_block, 0)
-        for p in range(GROUP):
-            col = slice(p * PAIR, (p + 1) * PAIR)
-            grad = jnp.where(low_half, dk[2 * p], dk[2 * p + 1])
-            raw_grad, gain_grad = pull_norm(k_ref[0, keys, col], grad, gain_ref[1:2, :])
+        grads = [jnp.where(low_half, dk[2 * p], dk[2 * p + 1]) for p in range(GROUP)]
+        raw_grads, gain_grads = pull_norm(
+            [k_ref[0, keys, col] for col in cols], grads, gain_ref[1:2, :]
+        )
+        for p, col in enumerate(cols):
+            raw_grad = raw_grads[p]
             out_ref[1, 0, keys, col] = raw_grad
-            stat_ref[0, 1:2, col] += gain_grad
+            stat_ref[0, 1:2, col] += gain_grads[p]
             stat_ref[0, 3:4, col] += jnp.sum(raw_grad.astype(f32), axis=0, keepdims=True)
             grad_v = jnp.where(low_half, dv[2 * p], dv[2 * p + 1]).astype(bf16)
             out_ref[2, 0, keys, col] = grad_v
@@ -235,12 +255,14 @@
 
     def finish(b, _):
         at = pl.ds(pl.multiple_of(b * BLK, BLK), BLK)
-        for p in range(GROUP):
-            col = slice(p * PAIR, (p + 1) * PAIR)
-            grad = dqt[p, :, at].T * 0.125
-            raw_grad, gain_grad = pull_norm(q_ref[0, at, col], grad, gain_ref[0:1, :])
+        grads = [dqt[p, :, at].T * 0.125 for p in range(GROUP)]
+        raw_grads, gain_grads = pull_norm(
+            [q_ref[0, at, col] for col in cols], grads, gain_ref[0:1, :]
+        )
+        for p, col in enumerate(cols):
+            raw_grad = raw_grads[p]
             out_ref[0, 0, at, col] = raw_grad
-            stat_ref[0, 0:1, col] += gain_grad
+            stat_ref[0, 0:1, col] += gain_grads[p]
             stat_ref[0, 2:3, col] += jnp.sum(raw_grad.astype(f32), axis=0, keepdims=True)
         return 0
 
@@ -417,38 +439,54 @@
 def gather_kernel(fsdp, replicas, pieces, *refs):
     count = len(pieces)
     shards, fulls = refs[:count], refs[count : 2 * count]
-    own_sem, out_send, out_recv, side_send, side_recv = refs[2 * count :]
+    own_sem, sends, recvs = refs[2 * count :]
     me = Place(fsdp, replicas)
     sibling = me.device(core=1 - me.core)
+    across = me.device(side=1 - me.side)
     peers = [lax.rem(me.f + k, fsdp) for k in range(1, fsdp)]
     sources = [lax.rem(me.f + fsdp - k, fsdp) for k in range(1, fsdp)]
-    greet([sibling] + [me.device(f=peer) for peer in peers])
-    own, outer, inner = [], [], []
+    greet([sibling, across] + [me.device(f=peer) for peer in peers])
+    outer, crossing, inner = [], [], []
     for i in range(count):
         for start, size in pieces[i]:
             col = pl.ds(start, size)
             for k, peer in enumerate(peers):
                 at = len(outer)
                 copy = remote(
-                    shards[i].at[me.core, :, col],
-                    fulls[i].at[me.f, me.core, :, col],
-                    out_send.at[at],
-                    out_recv.at[at],
+                    shards[i].at[me.side, me.core, :, col],
+                    fulls[i].at[me.f, me.side, me.core, :, col],
+                    sends.at[0, at],
+                    recvs.at[0, at],
                     me.device(f=peer),
                 )
                 copy.start()
                 outer.append((copy, i, col, k))
+    own = []
     for i in range(count):
         copy = pltpu.make_async_copy(shards[i], fulls[i].at[me.f], own_sem.at[i])
         copy.start()
         own.append(copy)
-    for at, (copy, i, col, k) in enumerate(outer):
-        copy.wait_recv()
-        landed = fulls[i].at[sources[k], me.core, :, col]
-        forward = remote(landed, landed, side_send.at[at], side_recv.at[at], sibling)
-        forward.start()
-        inner.append(forward)
-    for copy, *_ in outer:
+
+    def forward(landed, kind, at, device):
+        copy = remote(landed, landed, sends.at[kind, at], recvs.at[kind, at], device)
+        copy.start()
+        return copy
+
+    for at in range(len(outer) + 1):
+        if at < len(outer):
+            copy, i, col, k = outer[at]
+            copy.wait_recv()
+            landed = fulls[i].at[sources[k], me.side, me.core, :, col]
+            crossing.append(forward(landed, 1, at, across))
+            inner.append(forward(landed, 2, at, sibling))
+        if at > 0:
+            _unused, i, col, k = outer[at - 1]
+            crossing[at - 1].wait_recv()
+            landed = fulls[i].at[sources[k], 1 - me.side, me.core, :, col]
+            inner.append(forward(landed, 3, at - 1, sibling))
+    for copy, *_unused in outer:
+        copy.wait_send()
+    for copy in crossing:
         copy.wait_send()
     for copy in inner:
         copy.wait()
@@ -456,18 +494,20 @@
         copy.wait()
 
 
-def gather_halves(fsdp, replicas, shards, pieces):
+def gather_quarters(fsdp, replicas, shards, pieces):
     copies = sum(len(item) for item in pieces) * (fsdp - 1)
-    any_space = pl.BlockSpec(memory_space=pltpu.VMEM)
+    vmem = pl.BlockSpec(memory_space=pltpu.VMEM)
     return pl.pallas_call(
         functools.partial(gather_kernel, fsdp, replicas, pieces),
-        name="gather_halves",
-        in_specs=[any_space] * len(shards),
-        out_specs=[any_space] * len(shards),
+        name="gather_quarters",
+        in_specs=[vmem] * len(shards),
+        out_specs=[vmem] * len(shards),
         out_shape=[jax.ShapeDtypeStruct((fsdp,) + item.shape, item.dtype) for item in shards],
         scratch_shapes=[pltpu.SemaphoreType.DMA((len(shards),))]
-        + [pltpu.SemaphoreType.DMA((copies,))] * 4,
-        compiler_params=pltpu.CompilerParams(collective_id=1, has_side_effects=True),
+        + [pltpu.SemaphoreType.DMA((4, copies))] * 2,
+        compiler_params=pltpu.CompilerParams(
+            collective_id=1, has_side_effects=True, vmem_limit_bytes=32 << 20
+        ),
     )(*shards)
 
 
@@ -617,6 +657,83 @@
     return v * half, slope
 
 
+MLP_BLOCK = 512
+MLP_ROWS = 512
+
+
+def mlp_kernel(
+    n_ref, nt_ref, g_ref, gt_ref, wi_ref, wo_ref, b_ref,
+    y_ref, d_ref, gwi_ref, gwo_ref, gb_ref, act, dh,
+):
+    tokens, width = n_ref.shape
+
+    @pl.when(pl.program_id(0) == 0)
+    def _():
+        y_ref[...] = jnp.zeros_like(y_ref)
+        d_ref[...] = jnp.zeros_like(d_ref)
+
+    gb_ref[...] = jnp.zeros_like(gb_ref)
+
+    def first(i):
+        at = pl.ds(pl.multiple_of(i * MLP_ROWS, MLP_ROWS), MLP_ROWS)
+        return at, dot(n_ref[at, :], wi_ref[...]), dot_nt(g_ref[at, :], wo_ref[...])
+
+    def rows(i, _):
+        ahead = [first(i * 2)]
+        for j in range(2):
+            if j + 1 < 2:
+                ahead.append(first(i * 2 + j + 1))
+            at, hidden, pull = ahead[j]
+            activated, slope = gelu_both(hidden + b_ref[...])
+            activated = activated.astype(bf16)
+            grad = (pull * slope).astype(bf16)
+            act[at, :] = activated
+            dh[at, :] = grad
+            gb_ref[...] += jnp.sum(grad.astype(f32), axis=0, keepdims=True)
+            y_ref[at, :] += dot(activated, wo_ref[...])
+            d_ref[at, :] += dot_nt(grad, wi_ref[...])
+        return 0
+
+    lax.fori_loop(0, tokens // (MLP_ROWS * 2), rows, 0)
+    for r in range(0, width, 256):
+        at = slice(r, r + 256)
+        gwi_ref[at, :] = dot(nt_ref[at, :], dh[...]).astype(bf16)
+        gwo_ref[:, at] = dot(gt_ref[at, :], act[...]).astype(bf16).T
+
+
+def mlp(normed, grad, w_in, w_out, b_in):
+    tokens, width = normed.shape
+    hidden = w_in.shape[1]
+    steps = hidden // MLP_BLOCK
+    once = pl.Buffered(1)
+    tall = pl.BlockSpec((tokens, width), lambda i: (0, 0), pipeline_mode=once)
+    flat = pl.BlockSpec((width, tokens), lambda i: (0, 0), pipeline_mode=once)
+    into = pl.BlockSpec((width, MLP_BLOCK), lambda i: (0, i))
+    out_of = pl.BlockSpec((MLP_BLOCK, width), lambda i: (i, 0))
+    bias = pl.BlockSpec((1, MLP_BLOCK), lambda i: (0, i))
+    return pl.pallas_call(
+        mlp_kernel,
+        name="mlp_both_ways",
+        grid=(steps,),
+        in_specs=[tall, flat, tall, flat, into, out_of, bias],
+        out_specs=[tall, tall, into, out_of, bias],
+        out_shape=[
+            jax.ShapeDtypeStruct((tokens, width), f32),
+            jax.ShapeDtypeStruct((tokens, width), f32),
+            jax.ShapeDtypeStruct((width, hidden), bf16),
+            jax.ShapeDtypeStruct((hidden, width), bf16),
+            jax.ShapeDtypeStruct((1, hidden), f32),
+        ],
+        scratch_shapes=[pltpu.VMEM((tokens, MLP_BLOCK), bf16)] * 2,
+        cost_estimate=pl.CostEstimate(
+            flops=12 * tokens * width * hidden,
+            bytes_accessed=tokens * width * 16,
+            transcendentals=tokens * hidden,
+        ),
+        compiler_params=pltpu.CompilerParams(vmem_limit_bytes=58 << 20),
+    )(normed, normed.T, grad, grad.T, w_in, w_out, b_in.reshape(1, hidden))
+
+
 def on_device(fsdp, replicas, *args):
     (
         patches,
@@ -637,18 +754,23 @@
     tokens = rows * slots
     small = (ln_gain, ln_bias, b_qkv, qk_gain, out_bias, b_in)
     flat = jnp.concatenate([item.reshape(-1) for item in small])
-    small_cols = -(-flat.shape[0] // (32 * PAIR)) * PAIR
-    flat = jnp.pad(flat, (0, 32 * small_cols - flat.shape[0])).reshape(2, 16, small_cols)
+    small_cols = -(-flat.shape[0] // (64 * PAIR)) * PAIR
+    flat = jnp.pad(flat, (0, 64 * small_cols - flat.shape[0])).reshape(2, 2, 16, small_cols)
     shard_rows, columns = w_qkv.shape
     third = columns // 3
-    w_qkv_full, flat_full = gather_halves(
+    w_qkv_full, flat_full, w_out_full = gather_quarters(
         fsdp,
         replicas,
-        [w_qkv.reshape(2, shard_rows // 2, columns), flat],
-        [[(0, third), (third, third), (2 * third, third)], [(0, small_cols)]],
+        [w_qkv.reshape(2, 2, -1, columns), flat, w_out.reshape(2, 2, -1, width)],
+        [
+            [(0, third), (third, third), (2 * third, third)],
+            [(0, small_cols)],
+            [(0, width // 2), (width // 2, width // 2)],
+        ],
     )
     w_qkv_full = w_qkv_full.reshape(width, columns)
-    flat_full, w_proj, w_in, w_out = lax.optimization_barrier((flat_full, w_proj, w_in, w_out))
+    w_out_full = w_out_full.reshape(-1, width)
+    flat_full, w_proj, w_in = lax.optimization_barrier((flat_full, w_proj, w_in))
     flat_full = flat_full.reshape(fsdp, -1).astype(f32)
     full_small = []
     at = 0
@@ -660,7 +782,6 @@
     gains, shifts, b_qkv_full, qk_gain_full, out_bias_full, b_in_full = full_small
     w_proj_full = lax.all_gather(w_proj, "fsdp", axis=0, tiled=True)
     w_in_full = lax.all_gather(w_in, "fsdp", axis=0, tiled=True)
-    w_out_full = lax.all_gather(w_out, "fsdp", axis=0, tiled=True)
 
     pic, inside, bounds = picture_tables(lengths, slots)
     pic = pic[:, :, None]
@@ -679,18 +800,13 @@
     grad_y = cotangent.reshape(tokens, width).astype(f32) * inside
     grad_mlp = grad_y.astype(bf16)
 
-    hidden = dot(normed2, w_in_full) + b_in_full
-    activated, slope = gelu_both(hidden)
-    activated = activated.astype(bf16)
-    block_out = resid + dot(activated, w_out_full) + out_bias_full[1]
-    block_out = block_out.astype(bf16)
-    grad_hidden = (dot_nt(grad_mlp, w_out_full) * slope).astype(bf16)
+    branch, grad_norm2, grad_w_in, grad_w_out, grad_b_in = mlp(
+        normed2, grad_mlp, w_in_full, w_out_full, b_in_full
+    )
+    grad_b_in = grad_b_in[0]
+    block_out = (resid + branch + out_bias_full[1]).astype(bf16)
     tt = (((0,), (0,)), ((), ()))
-    grad_w_out = lax.dot_general(activated, grad_mlp, tt, preferred_element_type=f32).astype(bf16)
-    grad_w_in = lax.dot_general(normed2, grad_hidden, tt, preferred_element_type=f32).astype(bf16)
-    grad_b_in = jnp.sum(grad_hidden.astype(f32), axis=0)
     grad_bias_mlp = jnp.sum(grad_y, axis=0)
-    grad_norm2 = dot_nt(grad_hidden, w_in_full)
     back2, grad_gain2, grad_shift2 = norm_back(grad_norm2, n2, rstd2, gains[1])
     grad_resid = grad_y + back2
     grad_branch = grad_resid.astype(bf16)

time: 651 us -> 648 us (level)
  matrix products: 185 us -> 58.9 us
  local copies, waits for them, and re-layouts: 26.5 us -> 85.7 us
  Pallas kernels: 372 us -> 407 us
  other arithmetic: 36 us -> 70 us
  waiting for transfers between devices: 12 us -> 0.71 us
    pallas_call x1 -> x2, Pallas kernels: 28 us -> 122 us  [the longest x1 85.4 us: mlp(): pl.pallas_call(mlp_kernel, name='mlp_both_ways', grid=(steps,), in_specs=...]
    dot_general x6 -> x4, matrix products: 67.6 us -> 24.1 us  [dot_nt(): return lax.dot_general(a, b, NT, preferred_element_type=f32)]
    dot_general x4 -> x2, matrix products: 58.2 us -> 17 us  [dot(): return jnp.dot(a, b, preferred_element_type=f32)]
    dot_general x2 -> x0, matrix products: 41.2 us -> none  [the longest x1 21.3 us: on_device(): lax.dot_general(activated, grad_mlp, tt, preferred_element_type=f32)]
    pallas_call x1, Pallas kernels: 167 us -> 138 us  [reduce_everywhere(): pl.pallas_call(functools.partial(reduce_kernel, fsdp, replicas, count, ch...]
    convert_element_type x0 -> x4, local copies, waits for them, and re-layouts: none -> 17 us  [the longest x1 5.75 us: on_device(): source = patches.reshape(tokens, width).astype(f32)]
    unnamed x80, local copies, waits for them, and re-layouts: 6.34 us -> 22 us
    pallas_call x1, Pallas kernels: 63 us -> 48.1 us  [attention(): pl.pallas_call(forward_kernel, name='attention_forward', grid_spec=pltpu....]
  transfers between devices with their start and end apart: 3 -> 2, of which waited for: 1 -> 0; matrix products, arithmetic and copies ran while one was open for 11% -> 9% of each run, Pallas kernels for 10% -> 8%
where the time goes in v3:
time: 648 us; the launch traced here: 637 us
  Pallas kernels  407 us (63%)
  local copies, waits for them, and re-layouts  85.7 us (13%)
  other arithmetic  70 us (11%)
  matrix products  58.9 us (9%)
  between operations  14.9 us (2%)
    pallas_call x1, Pallas kernels, reduce_everywhere(): pl.pallas_call(functools.partial(reduce_kernel, fsdp, replicas, count, ch...  138 us
    pallas_call x1, Pallas kernels, attention_back(): pl.pallas_call(backward_kernel, name='attention_backward', grid_spec=pltp...  99.1 us
    pallas_call x1, Pallas kernels, mlp(): pl.pallas_call(mlp_kernel, name='mlp_both_ways', grid=(steps,), in_specs=...  85.4 us
    pallas_call x1, Pallas kernels, attention(): pl.pallas_call(forward_kernel, name='attention_forward', grid_spec=pltpu....  48.1 us
    pallas_call x1, Pallas kernels, gather_quarters(): pl.pallas_call(functools.partial(gather_kernel, fsdp, replicas, pieces),...  36.2 us
    dot_general x4, matrix products, dot_nt(): return lax.dot_general(a, b, NT, preferred_element_type=f32)  24.1 us
    unnamed x80, local copies, waits for them, and re-layouts  22 us
    dot_general x2, matrix products, dot(): return jnp.dot(a, b, preferred_element_type=f32)  17 us
  transfers between devices with their start and end apart: 2, of which 0 were waited for; matrix products, arithmetic and copies ran while one was open for 9% of the time, Pallas kernels for 8%

profile of v3, /device:TPU:1, one launch (start us, length us, event | category | flops | bytes accessed | tf_op | source)
XLA Modules:
  0.0 637.5 jit_solution(17213676862235065418)
XLA Ops:
  14.7 36.2 %gather_quarters.1 = (bf16[2,2,2,96,2304]{4,3,2,1,0:T(8,128)(2,1)S(1)}, bf16[2,2,2,16,128]{4,3,2,1,0:T(8,128)(2,1)S(1)}, bf16[2,2,2,384,768]{4,3,2,1,0:T(8,128)(2,1)S(1)}) custom-call(bf16[2,2,96,2304]{3,2,1,0:T(8,128)(2,1)S(1)} %bitcast.114, bf16[2,2,16,128]{3,2,1,0:T(8,128)(2,1)S(1)} %bitcast.119, bf16[2,2,384,768]{3,2,1,0:T(8,128)(2,1)S(1)} %bitcast.113), custom_call_target="tpu_custom_call" | custom-call | tf_op jit(solution)/shard_map/gather_quarters/pallas_call | solution.py:500
  59.9 5.8 fusion.31.gt_ref
  72.1 5.8 copy.103
  77.8 4.7 copy.88.g_ref
  88.2 9.7 %add_convert_fusion = bf16[2048,2304]{1,0:T(8,128)(2,1)} fusion(bf16[2048,768]{1,0:T(8,128)(2,1)S(1)} %bitcast.137, bf16[768,2304]{1,0:T(8,128)(2,1)S(1)} %bitcast.115, f32[2304]{0:T(1024)S(1)} %add.153), kind=kOutput, calls=%fused_computation | convolution fusion | flops 7257194496 | bytes 16131072 | tf_op jit(solution)/shard_map/dot_general | solution.py:24
  98.0 48.1 %attention_forward.1 = (bf16[2,1024,768]{2,1,0:T(8,128)(2,1)S(1)}, f32[2,1024,768]{2,1,0:T(8,128)}) custom-call(s32[2,4,4]{2,1,0:T(4,128)S(1)} %pad_add_fusion.bounds, bf16[2,1024,2304]{2,1,0:T(8,128)(2,1)} %bitcast.172, bf16[2,1024,2304]{2,1,0:T(8,128)(2,1)} %bitcast.173, bf16[2,1024,2304]{2,1,0:T(8,128)(2,1)} %bitcast.174, ...), custom_call_target="tpu_custom_call" | custom-call | flops 25769803776 | bytes 18874368 | tf_op jit(solution)/shard_map/attention_forward/pallas_call | solution.py:280
  147.8 7.2 %fusion.15 = (f32[2048]{0:T(1024)S(1)}, f32[2048,768]{0,1:T(8,128)S(1)}) fusion(f32[768]{0:T(1024)S(1)} %add.157, f32[2048,768]{0,1:T(8,128)} %copy.103, bf16[2048,768]{1,0:T(8,128)(2,1)} %bitcast.122, bf16[768,768]{1,0:T(8,128)(2,1)} %all-gather.3.cloned.1.call-done), kind=kOutput, calls=%fused_computation.95 | convolution fusion | flops 2420635648 | bytes 16919552 | tf_op jit(solution)/shard_map/dot_general | solution.py:24
  161.5 5.5 fusion.32.nt_ref
  166.9 85.4 %mlp_both_ways.1 = (f32[2048,768]{1,0:T(8,128)}, f32[2048,768]{1,0:T(8,128)}, bf16[768,3072]{1,0:T(8,128)(2,1)}, bf16[3072,768]{1,0:T(8,128)(2,1)}, f32[1,3072]{1,0:T(1,128)}) custom-call(bf16[2048,768]{1,0:T(8,128)(2,1)} %copy.87.n_ref, bf16[768,2048]{1,0:T(8,128)(2,1)} %fusion.32.nt_ref, bf16[2048,768]{1,0:T(8,128)(2,1)} %copy.88.g_ref, ...), custom_call_target="tpu_custom_call" | custom-call | flops 57982058496 | bytes 25165824 | tf_op jit(solution)/shard_map/mlp_both_ways/pallas_call | solution.py:714
  252.4 6.6 %copy.89 = f32[2048,768]{0,1:T(8,128)} copy(f32[2048,768]{1,0:T(8,128)} %get-tuple-element.41) | data formatting | bytes 12582912 | tf_op jit(solution)/shard_map/mlp_both_ways/pallas_call | solution.py:714
  259.0 6.6 %copy.90 = f32[2048,768]{0,1:T(8,128)} copy(f32[2048,768]{1,0:T(8,128)} %get-tuple-element.42) | data formatting | bytes 12582912 | tf_op jit(solution)/shard_map/mlp_both_ways/pallas_call | solution.py:714
  269.6 10.3 %multiply_reduce_fusion.1 = (bf16[768]{0:T(1024)(128)(2,1)}, f32[2048]{0:T(1024)S(1)}, f32[2048]{0:T(1024)S(1)}, bf16[2048,768]{0,1:T(8,128)(2,1)}) fusion(f32[2048,768]{0,1:T(8,128)} %copy.90, f32[2048,768]{0,1:T(8,128)} %copy-done.11, f32[2048]{0:T(1024)S(1)} %add_rsqrt_fusion, f32[2048]{0:T(1024)S(1)} %broadcast_multiply_fusion.4, f32[768]{0:T(1024)S(1)} %mul.150, ...), kind=kLoop, calls=%fused_computation.2 | loop fusion | flops 17296640 | bytes 22060544 | tf_op jit(solution)/shard_map/reduce_sum | solution.py:397
  280.2 5.8 convert_reduce_fusion.2
  289.7 4.1 convolution_convert_fusion
  293.9 99.1 %attention_backward.1 = (bf16[3,2,1024,768]{3,2,1,0:T(8,128)(2,1)}, f32[2,8,768]{2,1,0:T(8,128)}) custom-call(s32[2,4,4]{2,1,0:T(4,128)} %copy-done.6, bf16[2,1024,2304]{2,1,0:T(8,128)(2,1)} %bitcast.175, bf16[2,1024,2304]{2,1,0:T(8,128)(2,1)} %bitcast.176, bf16[2,1024,2304]{2,1,0:T(8,128)(2,1)} %bitcast.177, bf16[2,1024,768]{2,1,0:T(8,128)(2,1)} %copy-done.9, ...), custom_call_target="tpu_custom_call" | custom-call | flops 64424509440 | bytes 31457280 | tf_op jit(solution)/shard_map/attention_backward/pallas_call | solution.py:320
  394.9 5.8 fusion.12
  404.5 4.5 fusion.3
  412.7 4.5 fusion.1
  431.3 6.7 %convolution_convert_fusion.2 = bf16[768,768]{1,0:T(8,128)(2,1)} fusion(bf16[2048,768]{1,0:T(8,128)(2,1)} %bitcast.138, bf16[2048,768]{1,0:T(8,128)(2,1)} %bitcast.127), kind=kOutput, calls=%fused_computation.26 | convolution fusion | flops 2416508928 | bytes 7471104 | tf_op jit(solution)/shard_map/dot_general | solution.py:825
  438.1 11.0 %multiply_reduce_fusion.2 = (bf16[768]{0:T(1024)(128)(2,1)}, f32[2048]{0:T(1024)}, f32[2048]{0:T(1024)}, bf16[768]{0:T(1024)(128)(2,1)}, f32[2048,768]{0,1:T(8,128)}) fusion(f32[2048,768]{0,1:T(8,128)} %copy.103, f32[2048]{0:T(1024)S(1)} %copy-done.25, f32[2048]{0:T(1024)S(1)} %copy-done.26, f32[768]{0:T(1024)S(1)} %copy-done.28, ...), kind=kOutput, calls=%fused_computation.3 | convolution fusion | flops 2433214976 | bytes 29531136 | tf_op jit(solution)/shard_map/dot_general | solution.py:28
  454.2 138.4 %reduce_everywhere.1 = (bf16[4,2,2,96,768]{4,3,2,1,0:T(8,128)(2,1)}, bf16[4,2,2,24,3072]{4,3,2,1,0:T(8,128)(2,1)}, bf16[4,2,2,24,768]{4,3,2,1,0:T(8,128)(2,1)}, ...) custom-call(bf16[2,4,2,2,96,768]{5,4,3,2,1,0:T(8,128)(2,1)} %bitcast, ...), custom_call_target="tpu_custom_call" | custom-call | tf_op jit(solution)/shard_map/reduce_everywhere/pallas_call | solution.py:630
  597.1 9.8 %multiply_add_fusion = f32[2048,768]{0,1:T(8,128)} fusion(f32[2048,768]{0,1:T(8,128)} %copy-done.15, f32[2048,768]{0,1:T(8,128)} %get-tuple-element.132, f32[2048,768]{0,1:T(8,128)} %copy.103, f32[2048]{0:T(1024)S(1)} %broadcast_multiply_fusion, f32[2048]{0:T(1024)S(1)} %copy-done.25, f32[2048]{0:T(1024)S(1)} %broadcast_multiply_fusion.1, ...), kind=kLoop, calls=%fused_computation.4 | loop fusion | flops 12582912 | bytes 25201664 | tf_op jit(solution)/shard_map/add | solution.py:832
  606.9 6.7 %copy.106 = f32[2048,768]{1,0:T(8,128)} copy(f32[2048,768]{0,1:T(8,128)} %multiply_add_fusion) | data formatting | bytes 12582912
  620.9 4.6 bitcast_convert_fusion.1
  (177 shorter events, 89.7 us)
Async XLA Ops:
  7.2 48.4 %copy-start.32 = (s32[2,10]{1,0:T(2,128)S(1)}, s32[2,10]{1,0:T(2,128)}, u32[]{:S(2)}) copy-start(s32[2,10]{1,0:T(2,128)} %param.24) | copy-start | bytes 244
  7.2 140.6 %all-gather.3.cloned.1.call-start = ((), (), s32[]{:S(2)}) async-start(), calls=%async_computation | async-start | bytes 1769472 | tf_op jit(solution)/shard_map/all_gather | solution.py:783
  14.7 41.5 %copy-start.17 = (bf16[2,1024,768]{2,1,0:T(8,128)(2,1)S(1)}, bf16[2,1024,768]{2,1,0:T(8,128)(2,1)}, u32[]{:S(2)}) copy-start(bf16[2,1024,768]{2,1,0:T(8,128)(2,1)} %param.25) | copy-start | bytes 9437188
  54.9 112.1 %all-gather.5.cloned.1.call-start = ((), (), s32[]{:S(2)}) async-start(), calls=%async_computation.1 | async-start | bytes 7077888 | tf_op jit(solution)/shard_map/all_gather | solution.py:784
  72.1 25.9 %copy-start.2 = (s32[2,1024,1]{2,1,0:T(8,128)}, s32[2,1024,1]{2,1,0:T(8,128)S(1)}, u32[]{:S(2)}) copy-start(s32[2,1024,1]{2,1,0:T(8,128)S(1)} %copy.84.pic_ref) | copy-start | bytes 24580
  82.8 15.2 %copy-start.7 = (f32[2,128]{1,0:T(2,128)}, f32[2,128]{1,0:T(2,128)S(1)}, u32[]{:S(2)}) copy-start(f32[2,128]{1,0:T(2,128)S(1)} %pad_maximum_fusion.3.gain_ref) | copy-start | bytes 3076
  83.6 14.3 %copy-start.27 = (f32[768]{0:T(1024)}, f32[768]{0:T(1024)S(1)}, u32[]{:S(2)}) copy-start(f32[768]{0:T(1024)S(1)} %mul.144) | copy-start | bytes 9220
  84.3 13.6 %copy-start.6 = (s32[2,4,4]{2,1,0:T(4,128)}, s32[2,4,4]{2,1,0:T(4,128)S(1)}, u32[]{:S(2)}) copy-start(s32[2,4,4]{2,1,0:T(4,128)S(1)} %pad_add_fusion.bounds) | copy-start | bytes 388
  88.2 9.8 %copy-start.19 = (bf16[2,1024,768]{2,1,0:T(8,128)(2,1)}, bf16[2,1024,768]{2,1,0:T(8,128)(2,1)S(1)}, u32[]{:S(2)}) copy-start(bf16[2,1024,768]{2,1,0:T(8,128)(2,1)S(1)} %add_convert_fusion.3) | copy-start | bytes 9437188
  265.6 14.3 %slice-start = ((s8[6291456]{0:T(1024)(128)(4,1)}), s8[2097152]{0:T(1024)(128)(4,1)S(1)}, s32[]{:S(2)}) async-start(s8[6291456]{0:T(1024)(128)(4,1)} %bitcast.124), calls=%async_computation.2 | async-start | bytes 4194304
  269.6 10.3 %slice-start.1 = ((s8[6291456]{0:T(1024)(128)(4,1)}), s8[4194304]{0:T(1024)(128)(4,1)S(1)}, s32[]{:S(2)}) async-start(s8[6291456]{0:T(1024)(128)(4,1)} %bitcast.124), calls=%async_computation.3 | async-start | bytes 8388608
  269.6 10.6 %copy-start.13 = (f32[2048,768]{0,1:T(8,128)S(1)}, f32[2048,768]{0,1:T(8,128)}, u32[]{:S(2)}) copy-start(f32[2048,768]{0,1:T(8,128)} %copy.90) | copy-start | bytes 18874372
  280.2 5.8 copy-start.10
  417.1 20.9 %copy-start.25 = (f32[2048]{0:T(1024)S(1)}, f32[2048]{0:T(1024)}, u32[]{:S(2)}) copy-start(f32[2048]{0:T(1024)} %get-tuple-element.135) | copy-start | bytes 24580
  417.1 20.9 %copy-start.26 = (f32[2048]{0:T(1024)S(1)}, f32[2048]{0:T(1024)}, u32[]{:S(2)}) copy-start(f32[2048]{0:T(1024)} %get-tuple-element.136) | copy-start | bytes 24580
  431.3 6.7 %copy-start.16 = (bf16[1,2,1024,768]{3,2,1,0:T(8,128)(2,1)S(1)}, bf16[1,2,1024,768]{3,2,1,0:T(8,128)(2,1)}, u32[]{:S(2)}) copy-start(bf16[1,2,1024,768]{3,2,1,0:T(8,128)(2,1)} %get-tuple-element.114) | copy-start | bytes 9437188
  431.3 6.7 %copy-start.28 = (f32[768]{0:T(1024)S(1)}, f32[768]{0:T(1024)}, u32[]{:S(2)}) copy-start(f32[768]{0:T(1024)} %copy-done.27) | copy-start | bytes 9220
  454.2 142.9 %copy-start.31 = (f32[2048]{0:T(1024)S(1)}, f32[2048]{0:T(1024)}, u32[]{:S(2)}) copy-start(f32[2048]{0:T(1024)} %get-tuple-element.93) | copy-start | bytes 24580
  454.2 142.9 %copy-start.30 = (f32[2048]{0:T(1024)S(1)}, f32[2048]{0:T(1024)}, u32[]{:S(2)}) copy-start(f32[2048]{0:T(1024)} %get-tuple-element.97) | copy-start | bytes 24580
  454.2 142.9 %copy-start.29 = (f32[768]{0:T(1024)S(1)}, f32[768]{0:T(1024)}, u32[]{:S(2)}) copy-start(f32[768]{0:T(1024)} %copy-done.27) | copy-start | bytes 9220
  606.9 11.2 %copy-start.18 = (bf16[2048,768]{0,1:T(8,128)(2,1)S(1)}, bf16[2048,768]{0,1:T(8,128)(2,1)}, u32[]{:S(2)}) copy-start(bf16[2048,768]{0,1:T(8,128)(2,1)} %get-tuple-element.117) | copy-start | bytes 9437188
  620.9 7.3 %copy-start.22 = (bf16[4,2,2,24,768]{4,3,2,1,0:T(8,128)(2,1)S(1)}, bf16[4,2,2,24,768]{4,3,2,1,0:T(8,128)(2,1)}, u32[]{:S(2)}) copy-start(bf16[4,2,2,24,768]{4,3,2,1,0:T(8,128)(2,1)} %get-tuple-element.50) | copy-start | bytes 1769476
  620.9 7.3 %copy-start.23 = (bf16[4,2,2,24,768]{4,3,2,1,0:T(8,128)(2,1)S(1)}, bf16[4,2,2,24,768]{4,3,2,1,0:T(8,128)(2,1)}, u32[]{:S(2)}) copy-start(bf16[4,2,2,24,768]{4,3,2,1,0:T(8,128)(2,1)} %get-tuple-element.51) | copy-start | bytes 1769476
  620.9 7.3 %copy-start.24 = (bf16[4,2,2,24,768]{4,3,2,1,0:T(8,128)(2,1)S(1)}, bf16[4,2,2,24,768]{4,3,2,1,0:T(8,128)(2,1)}, u32[]{:S(2)}) copy-start(bf16[4,2,2,24,768]{4,3,2,1,0:T(8,128)(2,1)} %get-tuple-element.52) | copy-start | bytes 1769476
  (14 other events, 46.4 us)
Sparse Core Ops, SparseCore 0:
  55.0 21.5 all-gather.2
  78.1 62.6 all-gather.4

commit v4 on v3

--- a/solution.py
+++ b/solution.py
@@ -135,7 +135,9 @@
     lse_ref,
     pic_ref,
     gain_ref,
-    out_ref,
+    out_q,
+    out_k,
+    out_v,
     stat_ref,
     qa,
     ka,
@@ -243,11 +245,11 @@
         )
         for p, col in enumerate(cols):
             raw_grad = raw_grads[p]
-            out_ref[1, 0, keys, col] = raw_grad
+            out_k[0, keys, col] = raw_grad
             stat_ref[0, 1:2, col] += gain_grads[p]
             stat_ref[0, 3:4, col] += jnp.sum(raw_grad.astype(f32), axis=0, keepdims=True)
             grad_v = jnp.where(low_half, dv[2 * p], dv[2 * p + 1]).astype(bf16)
-            out_ref[2, 0, keys, col] = grad_v
+            out_v[0, keys, col] = grad_v
             stat_ref[0, 4:5, col] += jnp.sum(grad_v.astype(f32), axis=0, keepdims=True)
         return 0
 
@@ -261,7 +263,7 @@
         )
         for p, col in enumerate(cols):
             raw_grad = raw_grads[p]
-            out_ref[0, 0, at, col] = raw_grad
+            out_q[0, at, col] = raw_grad
             stat_ref[0, 0:1, col] += gain_grads[p]
             stat_ref[0, 2:3, col] += jnp.sum(raw_grad.astype(f32), axis=0, keepdims=True)
         return 0
@@ -334,7 +336,9 @@
                 pl.BlockSpec((2, PAIR), lambda r, g, b: (0, 0)),
             ],
             out_specs=[
-                pl.BlockSpec((3, 1, slots, wide), lambda r, g, b: (0, r, 0, g)),
+                whole,
+                whole,
+                whole,
                 pl.BlockSpec((1, 8, wide), lambda r, g, b: (r, 0, g)),
             ],
             scratch_shapes=[
@@ -349,7 +353,9 @@
             ],
         ),
         out_shape=[
-            jax.ShapeDtypeStruct((3, rows, slots, width), bf16),
+            jax.ShapeDtypeStruct((rows, slots, width), bf16),
+            jax.ShapeDtypeStruct((rows, slots, width), bf16),
+            jax.ShapeDtypeStruct((rows, slots, width), bf16),
             jax.ShapeDtypeStruct((rows, 8, width), f32),
         ],
         cost_estimate=pl.CostEstimate(
@@ -662,8 +668,8 @@
 
 
 def mlp_kernel(
-    n_ref, nt_ref, g_ref, gt_ref, wi_ref, wo_ref, b_ref,
-    y_ref, d_ref, gwi_ref, gwo_ref, gb_ref, act, dh,
+    n_ref, g_ref, wi_ref, wo_ref, b_ref,
+    y_ref, d_ref, gwi_ref, gwo_ref, gb_ref, act, dh, nt, gt,
 ):
     tokens, width = n_ref.shape
 
@@ -671,6 +677,14 @@
     def _():
         y_ref[...] = jnp.zeros_like(y_ref)
         d_ref[...] = jnp.zeros_like(d_ref)
+
+        def turn(i, _):
+            at = pl.ds(pl.multiple_of(i * 256, 256), 256)
+            nt[:, at] = n_ref[at, :].T
+            gt[:, at] = g_ref[at, :].T
+            return 0
+
+        lax.fori_loop(0, tokens // 256, turn, 0)
 
     gb_ref[...] = jnp.zeros_like(gb_ref)
 
@@ -697,8 +711,8 @@
     lax.fori_loop(0, tokens // (MLP_ROWS * 2), rows, 0)
     for r in range(0, width, 256):
         at = slice(r, r + 256)
-        gwi_ref[at, :] = dot(nt_ref[at, :], dh[...]).astype(bf16)
-        gwo_ref[:, at] = dot(gt_ref[at, :], act[...]).astype(bf16).T
+        gwi_ref[at, :] = dot(nt[at, :], dh[...]).astype(bf16)
+        gwo_ref[:, at] = dot(gt[at, :], act[...]).astype(bf16).T
 
 
 def mlp(normed, grad, w_in, w_out, b_in):
@@ -707,7 +721,6 @@
     steps = hidden // MLP_BLOCK
     once = pl.Buffered(1)
     tall = pl.BlockSpec((tokens, width), lambda i: (0, 0), pipeline_mode=once)
-    flat = pl.BlockSpec((width, tokens), lambda i: (0, 0), pipeline_mode=once)
     into = pl.BlockSpec((width, MLP_BLOCK), lambda i: (0, i))
     out_of = pl.BlockSpec((MLP_BLOCK, width), lambda i: (i, 0))
     bias = pl.BlockSpec((1, MLP_BLOCK), lambda i: (0, i))
@@ -715,7 +728,7 @@
         mlp_kernel,
         name="mlp_both_ways",
         grid=(steps,),
-        in_specs=[tall, flat, tall, flat, into, out_of, bias],
+        in_specs=[tall, tall, into, out_of, bias],
         out_specs=[tall, tall, into, out_of, bias],
         out_shape=[
             jax.ShapeDtypeStruct((tokens, width), f32),
@@ -724,14 +737,15 @@
             jax.ShapeDtypeStruct((hidden, width), bf16),
             jax.ShapeDtypeStruct((1, hidden), f32),
         ],
-        scratch_shapes=[pltpu.VMEM((tokens, MLP_BLOCK), bf16)] * 2,
+        scratch_shapes=[pltpu.VMEM((tokens, MLP_BLOCK), bf16)] * 2
+        + [pltpu.VMEM((width, tokens), bf16)] * 2,
         cost_estimate=pl.CostEstimate(
             flops=12 * tokens * width * hidden,
             bytes_accessed=tokens * width * 16,
             transcendentals=tokens * hidden,
         ),
         compiler_params=pltpu.CompilerParams(vmem_limit_bytes=58 << 20),
-    )(normed, normed.T, grad, grad.T, w_in, w_out, b_in.reshape(1, hidden))
+    )(normed, grad, w_in, w_out, b_in.reshape(1, hidden))
 
 
 def on_device(fsdp, replicas, *args):
@@ -814,13 +828,11 @@
     grad_attn = dot_nt(grad_branch, w_proj_full).astype(bf16)
     grad_w_proj = lax.dot_general(attn_flat, grad_branch, tt, preferred_element_type=f32).astype(bf16)
 
-    grad_qkv, stats = attention_back(
+    *grad_qkv, stats = attention_back(
         qkv, attn, grad_attn.reshape(rows, slots, width), lse, pic, bounds, pair_gain
     )
     stats = jnp.sum(stats, axis=0)
-    grad_qk_gain = jnp.sum(stats[0:2].reshape(2, H, HD), axis=1)
-    grad_b_qkv = stats[2:5].reshape(-1)
-    grad_qkv = grad_qkv.reshape(3, tokens, width)
+    grad_qkv = [item.reshape(tokens, width) for item in grad_qkv]
     grad_w_qkv = [
         lax.dot_general(normed1, grad_qkv[i], tt, preferred_element_type=f32).astype(bf16)
         for i in range(3)
@@ -831,29 +843,23 @@
     back1, grad_gain1, grad_shift1 = norm_back(grad_norm1, n1, rstd1, gains[0])
     grad_patches = (grad_resid + back1).reshape(rows, slots, width)
 
-    small_grads = (
-        jnp.stack([grad_gain1, grad_gain2]),
-        jnp.stack([grad_shift1, grad_shift2]),
-        grad_b_qkv,
-        grad_qk_gain,
+    lead = (fsdp, replicas // 4, 2, 2)
+    small_rows = [
+        stats[0:5],
+        jnp.stack([grad_gain1, grad_gain2, grad_shift1, grad_shift2]),
         jnp.stack([grad_bias_attn, grad_bias_mlp]),
-        grad_b_in,
-    )
-    flat_grads = jnp.concatenate(
-        [
-            jnp.moveaxis(item.reshape(item.shape[:-1] + (fsdp, -1)), -2, 0).reshape(fsdp, -1)
-            for item in small_grads
-        ],
-        axis=1,
-    ).astype(bf16)
-    lead = (fsdp, replicas // 4, 2, 2)
-    small_rows = 16
-    flat_grads = jnp.pad(
-        flat_grads, ((0, 0), (0, replicas * small_rows * PAIR - flat_grads.shape[1]))
+        grad_b_in.reshape(-1, width),
+    ]
+    small_rows = jnp.concatenate(small_rows, axis=0).astype(bf16)
+    row_count = small_rows.shape[0]
+    per_device = -(-row_count // replicas)
+    small_rows = jnp.pad(small_rows, ((0, replicas * per_device - row_count), (0, 0)))
+    small_rows = jnp.broadcast_to(
+        small_rows.reshape(lead[1:] + (per_device, width)), lead + (per_device, width)
     )
     payload = [grad_w_out, grad_w_in, *grad_w_qkv, grad_w_proj]
     payload = [item.reshape(lead + (-1, item.shape[-1])) for item in payload]
-    payload.append(flat_grads.reshape(lead + (small_rows, PAIR)))
+    payload.append(small_rows)
     whole = [(i, 0, item.shape[-2], 0, item.shape[-1]) for i, item in enumerate(payload)]
     out_half, in_half = whole[0][2] // 2, whole[1][4] // 2
     out_chunks = [[whole[0]]]
@@ -866,12 +872,21 @@
         item.reshape(-1, item.shape[-1]) for item in reduced[:6]
     )
     r_w_qkv = jnp.concatenate([r_q, r_k, r_v], axis=1)
-    r_flat = reduced[6].reshape(-1).astype(f32)
-    r_small = []
-    at = 0
-    for item in small:
-        r_small.append(r_flat[at : at + item.size].reshape(item.shape))
-        at += item.size
+    totals = reduced[6].reshape(-1, width)[:row_count].astype(f32)
+    group = lax.axis_index("fsdp")
+
+    def own(values):
+        size = values.shape[-1] // fsdp
+        return lax.dynamic_slice_in_dim(values, group * size, size, values.ndim - 1)
+
+    r_small = [
+        own(totals[5:7]),
+        own(totals[7:9]),
+        own(totals[2:5].reshape(-1)),
+        own(jnp.sum(totals[0:2].reshape(2, H, HD), axis=1)),
+        own(totals[9:11]),
+        own(totals[11:].reshape(-1)),
+    ]
     return (
         block_out.reshape(rows, slots, width),
         grad_patches,

time: 648 us -> 554 us (0.85); the launches traced: 637 us -> 550 us
  local copies, waits for them, and re-layouts: 85.7 us -> 22.5 us
  other arithmetic: 70 us -> 49 us
    convert_element_type x5 -> x0, local copies, waits for them, and re-layouts: 17.9 us -> none  [the longest x1 5.75 us: on_device(): source = patches.reshape(tokens, width).astype(f32)]
    pallas_call x2 -> x0, local copies, waits for them, and re-layouts: 13.2 us -> none  [mlp(): pl.pallas_call(mlp_kernel, name='mlp_both_ways', grid=(steps,), in_specs=...]
    transpose x2 -> x0, other arithmetic: 11.3 us -> none  [mlp(): return pl.pallas_call(mlp_kernel, name='mlp_both_ways', grid=(steps,), in...]
    unnamed x80 -> x78, local copies, waits for them, and re-layouts: 22 us -> 11.5 us
    pallas_call x1, Pallas kernels: 138 us -> 149 us  [reduce_everywhere(): pl.pallas_call(functools.partial(reduce_kernel, fsdp, replicas, count, ch...]
    slice x6 -> x3, local copies, waits for them, and re-layouts: 10.4 us -> 0.02 us  [the longest x1 0.01 us: on_device(): totals[9:11]]
    pallas_call x1, Pallas kernels: 99.1 us -> 91.1 us  [attention_back(): pl.pallas_call(backward_kernel, name='attention_backward', grid_spec=pltp...]
    another operation x6 -> x5, local copies, waits for them, and re-layouts: 6.56 us -> 0.04 us  [the longest x4 0.02 us: on_device(): jnp.stack([grad_gain1, grad_gain2, grad_shift1, grad_shift2])]
  transfers between devices with their start and end apart: 2 -> 2, of which waited for: 0 -> 1; matrix products, arithmetic and copies ran while one was open for 9% -> 6% of each run, Pallas kernels for 8% -> 8%
where the time goes in v4:
time: 554 us; the launch traced here: 550 us
  Pallas kernels  406 us (73%)
  matrix products  52.5 us (9%)
  other arithmetic  49 us (9%)
  local copies, waits for them, and re-layouts  22.5 us (4%)
  between operations  14.9 us (3%)
    pallas_call x1, Pallas kernels, reduce_everywhere(): pl.pallas_call(functools.partial(reduce_kernel, fsdp, replicas, count, ch...  149 us
    pallas_call x1, Pallas kernels, attention_back(): pl.pallas_call(backward_kernel, name='attention_backward', grid_spec=pltp...  91.1 us
    pallas_call x1, Pallas kernels, mlp(): pl.pallas_call(mlp_kernel, name='mlp_both_ways', grid=(steps,), in_specs=...  86.3 us
    pallas_call x1, Pallas kernels, attention(): pl.pallas_call(forward_kernel, name='attention_forward', grid_spec=pltpu....  43.6 us
    pallas_call x1, Pallas kernels, gather_quarters(): pl.pallas_call(functools.partial(gather_kernel, fsdp, replicas, pieces),...  36.2 us
    dot_general x4, matrix products, dot_nt(): return lax.dot_general(a, b, NT, preferred_element_type=f32)  19.4 us
    dot_general x2, matrix products, dot(): return jnp.dot(a, b, preferred_element_type=f32)  16.2 us
    dot_general x3, matrix products, on_device(): lax.dot_general(normed1, grad_qkv[i], tt, preferred_element_type=f32)  13.1 us
  transfers between devices with their start and end apart: 2, of which 1 were waited for; matrix products, arithmetic and copies ran while one was open for 6% of the time, Pallas kernels for 8%

profile of v4, /device:TPU:1, one launch (start us, length us, event | category | flops | bytes accessed | tf_op | source)
XLA Modules:
  0.0 550.4 jit_solution(15321649546184952761)
XLA Ops:
  14.7 36.2 %gather_quarters.1 = (bf16[2,2,2,96,2304]{4,3,2,1,0:T(8,128)(2,1)S(1)}, bf16[2,2,2,16,128]{4,3,2,1,0:T(8,128)(2,1)S(1)}, bf16[2,2,2,384,768]{4,3,2,1,0:T(8,128)(2,1)S(1)}) custom-call(bf16[2,2,96,2304]{3,2,1,0:T(8,128)(2,1)S(1)} %bitcast.125, bf16[2,2,16,128]{3,2,1,0:T(8,128)(2,1)S(1)} %bitcast.126, bf16[2,2,384,768]{3,2,1,0:T(8,128)(2,1)S(1)} %bitcast.124), custom_call_target="tpu_custom_call" | custom-call | tf_op jit(solution)/shard_map/gather_quarters/pallas_call | solution.py:506
  60.0 4.8 fusion.16.g_ref
  66.6 3.1 fusion.5
  69.7 9.9 %add_convert_fusion = bf16[2048,2304]{1,0:T(8,128)(2,1)} fusion(bf16[2048,768]{1,0:T(8,128)(2,1)S(1)} %bitcast.140, bf16[768,2304]{1,0:T(8,128)(2,1)S(1)} %bitcast.129, f32[2304]{0:T(1024)S(1)} %add.167), kind=kOutput, calls=%fused_computation | convolution fusion | flops 7257194496 | bytes 16131072 | tf_op jit(solution)/shard_map/dot_general | solution.py:24
  79.6 43.6 %attention_forward.1 = (bf16[2,1024,768]{2,1,0:T(8,128)(2,1)S(1)}, f32[2,1024,768]{2,1,0:T(8,128)}) custom-call(s32[2,4,4]{2,1,0:T(4,128)S(1)} %pad_add_fusion.bounds, bf16[2,1024,2304]{2,1,0:T(8,128)(2,1)} %bitcast.164, bf16[2,1024,2304]{2,1,0:T(8,128)(2,1)} %bitcast.165, bf16[2,1024,2304]{2,1,0:T(8,128)(2,1)} %bitcast.166, ...), custom_call_target="tpu_custom_call" | custom-call | flops 25769803776 | bytes 18874368 | tf_op jit(solution)/shard_map/attention_forward/pallas_call | solution.py:282
  124.9 6.3 %fusion.31 = (f32[2048]{0:T(1024)S(1)}, f32[2048,768]{1,0:T(8,128)S(1)}) fusion(f32[768]{0:T(1024)S(1)} %add.171, bf16[2048,768]{1,0:T(8,128)(2,1)} %bitcast.133, bf16[768,768]{1,0:T(8,128)(2,1)} %all-gather.3.cloned.1.call-done, bf16[2,1024,768]{2,1,0:T(8,128)(2,1)} %param.13), kind=kOutput, calls=%fused_computation.107 | convolution fusion | flops 2422208512 | bytes 13773824 | tf_op jit(solution)/shard_map/dot_general | solution.py:24
  136.1 4.6 all-gather.5.cloned.1.call-done.wi_ref
  140.7 86.3 %mlp_both_ways.1 = (f32[2048,768]{1,0:T(8,128)}, f32[2048,768]{1,0:T(8,128)}, bf16[768,3072]{1,0:T(8,128)(2,1)}, bf16[3072,768]{1,0:T(8,128)(2,1)}, f32[1,3072]{1,0:T(1,128)}) custom-call(bf16[2048,768]{1,0:T(8,128)(2,1)} %add_convert_fusion.2.n_ref, bf16[2048,768]{1,0:T(8,128)(2,1)} %fusion.16.g_ref, bf16[768,3072]{1,0:T(8,128)(2,1)} %all-gather.5.cloned.1.call-done.wi_ref, ...), custom_call_target="tpu_custom_call" | custom-call | flops 57982058496 | bytes 25165824 | tf_op jit(solution)/shard_map/mlp_both_ways/pallas_call | solution.py:727
  227.1 9.6 %multiply_reduce_fusion.1 = (bf16[768]{0:T(1024)(128)(2,1)S(1)}, f32[2048]{0:T(1024)S(1)}, f32[2048]{0:T(1024)S(1)}, bf16[768]{0:T(1024)(128)(2,1)S(1)}, bf16[2048,768]{1,0:T(8,128)(2,1)}) fusion(f32[2048,768]{1,0:T(8,128)} %get-tuple-element.44, f32[2048,768]{1,0:T(8,128)} %copy-done.11, f32[2048]{0:T(1024)S(1)} %add_rsqrt_fusion, ...), kind=kLoop, calls=%fused_computation.23 | loop fusion | flops 18868736 | bytes 22062080 | tf_op jit(solution)/shard_map/reduce_sum | solution.py:403
  236.8 6.7 %convert_reduce_fusion.2 = (bf16[768]{0:T(1024)(128)(2,1)S(1)}, f32[2048,768]{1,0:T(8,128)S(1)}) fusion(f32[2048]{0:T(1024)S(1)} %broadcast_multiply_fusion.2, f32[2048,768]{1,0:T(8,128)} %copy-done.11, f32[2048]{0:T(1024)S(1)} %broadcast_multiply_fusion.4, f32[2048]{0:T(1024)S(1)} %broadcast_multiply_fusion.3, f32[2048,768]{1,0:T(8,128)} %get-tuple-element.44, ...), kind=kLoop, calls=%fused_computation.99 | loop fusion | flops 18873600 | bytes 22065664 | tf_op jit(solution)/shard_map/reduce_sum | solution.py:827
  243.6 3.8 convolution_convert_fusion.1
  247.4 4.0 convolution_convert_fusion
  251.4 91.1 %attention_backward.1 = (bf16[2,1024,768]{2,1,0:T(8,128)(2,1)}, bf16[2,1024,768]{2,1,0:T(8,128)(2,1)}, bf16[2,1024,768]{2,1,0:T(8,128)(2,1)}, f32[2,8,768]{2,1,0:T(8,128)}) custom-call(s32[2,4,4]{2,1,0:T(4,128)} %copy-done.3, bf16[2,1024,2304]{2,1,0:T(8,128)(2,1)} %bitcast.167, bf16[2,1024,2304]{2,1,0:T(8,128)(2,1)} %bitcast.168, ...), custom_call_target="tpu_custom_call" | custom-call | flops 64424509440 | bytes 31457280 | tf_op jit(solution)/shard_map/attention_backward/pallas_call | solution.py:322
  342.6 5.7 %bitcast_convert_fusion.4 = bf16[768,768]{1,0:T(8,128)(2,1)} fusion(bf16[2,1024,768]{2,1,0:T(8,128)(2,1)S(1)} %copy-done.18, bf16[2,1024,768]{2,1,0:T(8,128)(2,1)} %get-tuple-element.46), kind=kOutput, calls=%fused_computation.39 | convolution fusion | flops 2416508928 | bytes 7471104 | tf_op jit(solution)/shard_map/dot_general | solution.py:837
  348.3 3.7 bitcast_convert_fusion.3
  352.0 3.7 bitcast_convert_fusion.2
  355.7 2.6 fusion.18
  358.4 4.5 fusion.20
  363.0 8.2 %fusion.15 = (bf16[768]{0:T(1024)(128)(2,1)S(1)}, f32[2048]{0:T(1024)S(1)}, f32[2048]{0:T(1024)S(1)}, bf16[768]{0:T(1024)(128)(2,1)S(1)}, f32[2048,768]{1,0:T(8,128)}) fusion(bf16[2,1024,768]{2,1,0:T(8,128)(2,1)S(1)} %copy-done.13, f32[2048]{0:T(1024)S(1)} %copy-done.26, f32[2048]{0:T(1024)S(1)} %copy-done.27, f32[768]{0:T(1024)S(1)} %copy-done.25, ...), kind=kOutput, calls=%fused_computation.21 | convolution fusion | flops 2434787840 | bytes 26385408 | tf_op jit(solution)/shard_map/dot_general | solution.py:28
  372.0 148.8 %reduce_everywhere.1 = (bf16[4,2,2,96,768]{4,3,2,1,0:T(8,128)(2,1)}, bf16[4,2,2,24,3072]{4,3,2,1,0:T(8,128)(2,1)}, bf16[4,2,2,24,768]{4,3,2,1,0:T(8,128)(2,1)}, ...) custom-call(bf16[2,4,2,2,96,768]{5,4,3,2,1,0:T(8,128)(2,1)} %bitcast, ...), custom_call_target="tpu_custom_call" | custom-call | tf_op jit(solution)/shard_map/reduce_everywhere/pallas_call | solution.py:636
  523.8 2.3 bitcast_convert_fusion.5
  526.1 4.6 bitcast_convert_fusion.1
  530.8 2.7 bitcast_convert_fusion
  535.5 5.8 %fusion.14 = f32[2048,768]{1,0:T(8,128)} fusion(f32[2048,768]{1,0:T(8,128)} %copy-done.16, bf16[2,1024,768]{2,1,0:T(8,128)(2,1)S(1)} %copy-done.13, f32[2048,768]{1,0:T(8,128)S(1)} %bitcast.136, f32[2048]{0:T(1024)S(1)} %broadcast_multiply_fusion, f32[2048]{0:T(1024)S(1)} %copy-done.26, f32[2048]{0:T(1024)S(1)} %broadcast_multiply_fusion.1, ...), kind=kLoop, calls=%fused_computation.20 | loop fusion | flops 14155776 | bytes 22055936 | tf_op jit(solution)/shard_map/add | solution.py:844
  (165 shorter events, 32.8 us)
Async XLA Ops:
  7.2 48.4 %copy-start.30 = (s32[2,10]{1,0:T(2,128)S(1)}, s32[2,10]{1,0:T(2,128)}, u32[]{:S(2)}) copy-start(s32[2,10]{1,0:T(2,128)} %param.24) | copy-start | bytes 244
  7.2 117.7 %all-gather.3.cloned.1.call-start = ((), (), s32[]{:S(2)}) async-start(), calls=%async_computation | async-start | bytes 1769472 | tf_op jit(solution)/shard_map/all_gather | solution.py:797
  14.7 42.0 %copy-start.12 = (bf16[2,1024,768]{2,1,0:T(8,128)(2,1)S(1)}, bf16[2,1024,768]{2,1,0:T(8,128)(2,1)}, u32[]{:S(2)}) copy-start(bf16[2,1024,768]{2,1,0:T(8,128)(2,1)} %param.13) | copy-start | bytes 9437188
  54.9 85.9 %all-gather.5.cloned.1.call-start = ((), (), s32[]{:S(2)}) async-start(), calls=%async_computation.1 | async-start | bytes 7077888 | tf_op jit(solution)/shard_map/all_gather | solution.py:798
  60.0 19.6 %copy-start.2 = (s32[2,1024,1]{2,1,0:T(8,128)}, s32[2,1024,1]{2,1,0:T(8,128)S(1)}, u32[]{:S(2)}) copy-start(s32[2,1024,1]{2,1,0:T(8,128)S(1)} %copy.61.pic_ref) | copy-start | bytes 24580
  65.0 14.6 %copy-start.4 = (f32[2,128]{1,0:T(2,128)}, f32[2,128]{1,0:T(2,128)S(1)}, u32[]{:S(2)}) copy-start(f32[2,128]{1,0:T(2,128)S(1)} %pad_maximum_fusion.gain_ref) | copy-start | bytes 3076
  65.9 13.7 %copy-start.24 = (f32[768]{0:T(1024)}, f32[768]{0:T(1024)S(1)}, u32[]{:S(2)}) copy-start(f32[768]{0:T(1024)S(1)} %mul.158) | copy-start | bytes 9220
  66.6 13.0 %copy-start.3 = (s32[2,4,4]{2,1,0:T(4,128)}, s32[2,4,4]{2,1,0:T(4,128)S(1)}, u32[]{:S(2)}) copy-start(s32[2,4,4]{2,1,0:T(4,128)S(1)} %pad_add_fusion.bounds) | copy-start | bytes 388
  69.7 9.9 %copy-start.17 = (bf16[2,1024,768]{2,1,0:T(8,128)(2,1)}, bf16[2,1024,768]{2,1,0:T(8,128)(2,1)S(1)}, u32[]{:S(2)}) copy-start(bf16[2,1024,768]{2,1,0:T(8,128)(2,1)S(1)} %fusion.5) | copy-start | bytes 9437188
  227.1 9.6 %copy-start.28 = (f32[1,3072]{1,0:T(1,128)S(1)}, f32[1,3072]{1,0:T(1,128)}, u32[]{:S(2)}) copy-start(f32[1,3072]{1,0:T(1,128)} %get-tuple-element.52) | copy-start | bytes 36868
  227.1 9.7 %copy-start.15 = (bf16[2,1024,768]{2,1,0:T(8,128)(2,1)S(1)}, bf16[2,1024,768]{2,1,0:T(8,128)(2,1)}, u32[]{:S(2)}) copy-start(bf16[2,1024,768]{2,1,0:T(8,128)(2,1)} %param.25) | copy-start | bytes 9437188
  236.8 6.8 %copy-start.10 = (bf16[2,1024,768]{2,1,0:T(8,128)(2,1)S(1)}, bf16[2,1024,768]{2,1,0:T(8,128)(2,1)}, u32[]{:S(2)}) copy-start(bf16[2,1024,768]{2,1,0:T(8,128)(2,1)} %copy-done.9) | copy-start | bytes 9437188
  251.4 91.2 %copy-start.18 = (bf16[2,1024,768]{2,1,0:T(8,128)(2,1)S(1)}, bf16[2,1024,768]{2,1,0:T(8,128)(2,1)}, u32[]{:S(2)}) copy-start(bf16[2,1024,768]{2,1,0:T(8,128)(2,1)} %copy-done.17) | copy-start | bytes 9437188
  342.6 5.7 %copy-start.34 = (bf16[2,1024,768]{2,1,0:T(8,128)(2,1)S(1)}, bf16[2,1024,768]{2,1,0:T(8,128)(2,1)}, u32[]{:S(2)}) copy-start(bf16[2,1024,768]{2,1,0:T(8,128)(2,1)} %get-tuple-element.47) | copy-start | bytes 9437188
  358.4 4.6 copy-start.13
  358.4 4.6 copy-start.25
  363.0 8.2 %copy-start.23 = (f32[2,8,768]{2,1,0:T(8,128)S(1)}, f32[2,8,768]{2,1,0:T(8,128)}, u32[]{:S(2)}) copy-start(f32[2,8,768]{2,1,0:T(8,128)} %get-tuple-element.51) | copy-start | bytes 147460
  363.0 8.2 %copy-start.29 = (bf16[1,768]{1,0:T(2,128)(2,1)S(1)}, bf16[1,768]{1,0:T(2,128)(2,1)}, u32[]{:S(2)}) copy-start(bf16[1,768]{1,0:T(2,128)(2,1)} %stack.37) | copy-start | bytes 4612
  523.8 6.9 %copy-start.19 = (bf16[4,2,2,96,768]{4,3,2,1,0:T(8,128)(2,1)S(1)}, bf16[4,2,2,96,768]{4,3,2,1,0:T(8,128)(2,1)}, u32[]{:S(2)}) copy-start(bf16[4,2,2,96,768]{4,3,2,1,0:T(8,128)(2,1)} %get-tuple-element.59) | copy-start | bytes 7077892
  523.8 11.6 %slice-start = ((s8[6291456]{0:T(1024)(128)(4,1)}), s8[4194304]{0:T(1024)(128)(4,1)S(1)}, s32[]{:S(2)}) async-start(s8[6291456]{0:T(1024)(128)(4,1)} %bitcast.135), calls=%async_computation.2 | async-start | bytes 8388608
  526.1 9.3 %slice-start.1 = ((s8[6291456]{0:T(1024)(128)(4,1)}), s8[2097152]{0:T(1024)(128)(4,1)S(1)}, s32[]{:S(2)}) async-start(s8[6291456]{0:T(1024)(128)(4,1)} %bitcast.135), calls=%async_computation.3 | async-start | bytes 4194304
  535.4 5.8 %copy-start.20 = (bf16[4,2,2,24,768]{4,3,2,1,0:T(8,128)(2,1)S(1)}, bf16[4,2,2,24,768]{4,3,2,1,0:T(8,128)(2,1)}, u32[]{:S(2)}) copy-start(bf16[4,2,2,24,768]{4,3,2,1,0:T(8,128)(2,1)} %get-tuple-element.54) | copy-start | bytes 1769476
  535.4 5.8 %copy-start.21 = (bf16[4,2,2,24,768]{4,3,2,1,0:T(8,128)(2,1)S(1)}, bf16[4,2,2,24,768]{4,3,2,1,0:T(8,128)(2,1)}, u32[]{:S(2)}) copy-start(bf16[4,2,2,24,768]{4,3,2,1,0:T(8,128)(2,1)} %get-tuple-element.55) | copy-start | bytes 1769476
  535.4 5.8 %copy-start.22 = (bf16[4,2,2,24,768]{4,3,2,1,0:T(8,128)(2,1)S(1)}, bf16[4,2,2,24,768]{4,3,2,1,0:T(8,128)(2,1)}, u32[]{:S(2)}) copy-start(bf16[4,2,2,24,768]{4,3,2,1,0:T(8,128)(2,1)} %get-tuple-element.56) | copy-start | bytes 1769476
  (15 other events, 44.1 us)
Sparse Core Ops, SparseCore 0:
  55.0 21.5 all-gather.2
  78.1 62.6 all-gather.4
